TPU v7x, 128 devices: a whole 4x4x4 slice. The times are simulated.
128 devices in a mesh: ga: 32 (over z, y, core), ba: 4 (over x).
Axes of the slice: x: 4, y: 4, z: 4, core: 2. Of those that a mesh axis runs over, the one named last changes fastest.
Arguments:
- coefficients: bfloat16 [40960, 6144], P('ga', 'ba')
- rotation: bfloat16 [6144, 6144], P('ga', 'ba'), may hold values from -0.078125 to 0.078125
Outputs:
- new_coefficients: bfloat16 [40960, 6144], P('ga', 'ba')
- band_rms: float32 [6144], P('ba')
All inputs are finite; a program needn't handle non-finite values.
Results may differ from a plain program's by a relative error of at most 0.0004.
Values may be sent and summed in bfloat16 or wider, within the bound.
A program may use at most 128 MiB of HBM per device.

v0:
```python
import jax
import jax.numpy as jnp
from jax import lax
from jax.sharding import PartitionSpec as P


def copy_for_each(array, axis):
    copies = jnp.broadcast_to(array, (lax.axis_size(axis), *array.shape))
    return lax.all_to_all(copies, axis, split_axis=0, concat_axis=0, tiled=True)


def joined_along(blocks, dim):
    shape = list(blocks.shape[1:])
    shape[dim] *= blocks.shape[0]
    return jnp.moveaxis(blocks, 0, dim).reshape(shape)


def gather_directly(array, axis, dim):
    blocks = copy_for_each(array, axis)
    return joined_along(blocks, dim)


def over_copies(array, axis):
    everything = copy_for_each(array, axis)
    return jnp.sum(everything, axis=0)


def body(coefficients, rotation):
    column_block = lax.all_gather(rotation, "ga", axis=0, tiled=True)
    rotated = jnp.dot(
        gather_directly(coefficients, "ba", 1), column_block, preferred_element_type=jnp.float32
    )
    squares = over_copies(jnp.sum(rotated * rotated, axis=0), "ga")
    total_rows = coefficients.shape[0] * lax.axis_size("ga")
    band_rms = jnp.sqrt(squares / total_rows + 1e-06)
    return ((rotated / band_rms).astype(jnp.bfloat16), band_rms)


def solution(mesh):
    in_specs = (P("ga", "ba"), P("ga", "ba"))
    out_specs = (P("ga", "ba"), P("ba"))
    return jax.shard_map(body, mesh=mesh, in_specs=in_specs, out_specs=out_specs, check_vma=False)
```

profile of v0, /device:TPU:1, one launch (start us, length us, event | category | flops | bytes accessed | tf_op | source)
XLA Modules:
  0.0 259.9 jit_solution(9544626655196929457)
XLA Ops:
  7.2 0.0 all-gather.2.cloned.1.call-start
  7.2 0.7 all-gather.2.cloned.1.call-update
  7.9 6.3 %copy.6 = bf16[1280,1536]{0,1:T(8,128)(2,1)} copy(bf16[1280,1536]{1,0:T(8,128)(2,1)} %param.2) | data formatting | bytes 7864320 | tf_op args[0]
  14.2 3.8 %broadcast_in_dim.7 = bf16[4,1280,1536]{1,2,0:T(8,128)(2,1)S(1)} broadcast(bf16[1280,1536]{0,1:T(8,128)(2,1)} %copy.6), dimensions={1,2} | broadcast | bytes 19660800 | tf_op jit(solution)/shard_map/broadcast_in_dim | solution.py:8
  17.9 176.6 %all_to_all.11 = bf16[4,1280,1536]{1,2,0:T(8,128)(2,1)} all-to-all(bf16[4,1280,1536]{1,2,0:T(8,128)(2,1)S(1)} %broadcast_in_dim.7), channel_id=1, replica_groups=mesh['ga'=32,'ba'=4] {'ba'}, dimensions={0} | all-to-all | bytes 31457280 | tf_op jit(solution)/shard_map/all_to_all | solution.py:9
  194.5 0.0 all-gather.2.cloned.1.call-done
  194.5 34.0 %multiply_reduce_fusion = (f32[1536]{0:T(1024)S(1)}, f32[1280,1536]{1,0:T(8,128)}) fusion(bf16[1280,6144]{0,1:T(8,128)(2,1)} %bitcast.5, bf16[6144,1536]{1,0:T(8,128)(2,1)} %all-gather.2.cloned.1.call-done), kind=kOutput, calls=%fused_computation.1 | convolution fusion | flops 24163121152 | bytes 42473472 | tf_op jit(solution)/shard_map/dot_general | solution.py:30
  228.5 0.1 broadcast_in_dim.8
  228.6 18.1 %all_to_all.12 = f32[32,1,1536]{2,1,0:T(1,128)S(1)} all-to-all(f32[32,1,1536]{2,1,0:T(1,128)S(1)} %broadcast_in_dim.8), channel_id=1, replica_groups=mesh['ga'=32,'ba'=4] {'ga'}, dimensions={0} | all-to-all | bytes 393216 | tf_op jit(solution)/shard_map/all_to_all | solution.py:9
  246.7 0.1 reduce_sum.19
  246.9 0.0 copy-start
  246.9 6.2 %divide_convert_fusion = bf16[1280,1536]{1,0:T(8,128)(2,1)} fusion(f32[1280,1536]{1,0:T(8,128)} %get-tuple-element.3, f32[1536]{0:T(1024)S(1)} %add_sqrt_fusion), kind=kLoop, calls=%fused_computation | loop fusion | flops 3932160 | bytes 11802624 | tf_op jit(solution)/shard_map/convert_element_type | solution.py:36
  253.1 0.0 copy-done
  (1 shorter events, 0.0 us)
Async XLA Ops:
  7.2 187.3 %all-gather.2.cloned.1.call-start = ((), (), s32[]{:S(2)}) async-start(), calls=%async_computation.2 | async-start | bytes 19464192 | tf_op jit(solution)/shard_map/all_gather | solution.py:29
  246.9 6.2 %copy-start = (f32[1536]{0:T(1024)}, f32[1536]{0:T(1024)S(1)}, u32[]{:S(2)}) copy-start(f32[1536]{0:T(1024)S(1)} %add_sqrt_fusion) | copy-start | bytes 18436
Sparse Core Ops, SparseCore 0:
  10.2 81.1 all-gather.1
where the time goes:
time: 260 us
  blocking collectives  195 us (75%)
  matrix products  34 us (13%)
  between operations  14 us (5%)
  local copies, waits for them, and re-layouts  10.1 us (4%)
  other arithmetic  6.32 us (2%)
    all_to_all x2, blocking collectives, copy_for_each(): return lax.all_to_all(copies, axis, split_axis=0, concat_axis=0, tiled=True)  195 us
    dot_general x1, matrix products, body(): jnp.dot(gather_directly(coefficients, 'ba', 1), column_block, preferred_e...  34 us
    unnamed x3, local copies, waits for them, and re-layouts  6.27 us
    convert_element_type x1, other arithmetic, body(): return ((rotated / band_rms).astype(jnp.bfloat16), band_rms)  6.18 us
  transfers between devices with their start and end apart: 1, of which 0 were waited for; matrix products, arithmetic and copies ran while one was open for 4% of the time, Pallas kernels for 0%

commit v1 on v0

v1 whole, which is shorter than its diff:
```python
import functools

import jax
import jax.numpy as jnp
from jax import lax
from jax.experimental import pallas as pl
from jax.experimental.pallas import tpu as pltpu
from jax.sharding import PartitionSpec as P

MESH = pl.DeviceIdType.MESH
SIDE = 4
CHUNKS = 8
TILE_M = 320
TILE_N = 512
TOTAL_ROWS = 40960


def kernel(
    coef, rot, out, rms_out, a_buf, r_buf, c_buf, sq_sum, sq_buf,
    load_sem, a_send, a_recv, r_send, r_recv, p_send, p_recv, s_send, s_recv, out_sem,
):
    rows, depth = coef.shape
    piece, cols = rot.shape
    peers = 2 * SIDE * SIDE
    chunk = rows // CHUNKS
    half_chunk = chunk // 2
    half = piece // 2
    quarter = half // 2

    g = lax.axis_index("ga")
    x = lax.axis_index("ba")
    core = g % 2
    y = (g // 2) % SIDE
    z = g // (2 * SIDE)
    sends = []

    def shift(value, by):
        return (value + by + SIDE) % SIDE

    def a_rows(block, start, size):
        return a_buf.at[block, pl.ds(start, size), :]

    def r_rows(zz, yy, cc, start, size):
        return r_buf.at[zz, pl.ds(pl.multiple_of((yy * 2 + cc) * piece + start, 16), size), :]

    own_rot = pltpu.make_async_copy(rot, r_rows(z, y, core, 0, piece), load_sem.at[CHUNKS])
    own_rot.start()
    own_coef = []
    for c in range(CHUNKS):
        copy = pltpu.make_async_copy(
            coef.at[pl.ds(c * chunk, chunk), :], a_rows(x, c * chunk, chunk), load_sem.at[c]
        )
        copy.start()
        own_coef.append(copy)

    barrier = pltpu.get_barrier_semaphore()

    def greet(step, carry):
        pl.semaphore_signal(
            barrier, inc=1, device_id={"ga": (g + step) % peers, "ba": x}, device_id_type=MESH
        )
        return carry

    lax.fori_loop(1, peers, greet, 0)
    for by in (1, -1):
        pl.semaphore_signal(
            barrier, inc=1, device_id={"ga": g, "ba": shift(x, by)}, device_id_type=MESH
        )
    pl.semaphore_wait(barrier, peers + 1)

    def remote(ref, send, recv, ga, ba):
        return pltpu.make_async_remote_copy(
            src_ref=ref, dst_ref=ref, send_sem=send, recv_sem=recv,
            device_id={"ga": ga, "ba": ba}, device_id_type=MESH,
        )

    def launch(copy):
        copy.start()
        sends.append(copy)

    def a_copy(direction, kind, c):
        by = 1 if direction == 0 else -1
        if kind == 0:
            ref = a_rows(x, c * chunk, chunk)
        else:
            ref = a_rows(shift(x, -by), c * chunk + direction * half_chunk, half_chunk)
        return remote(ref, a_send.at[direction, kind, c], a_recv.at[direction, kind, c], g, shift(x, by))

    def a_arrived(direction, kind, c):
        by = 1 if direction == 0 else -1
        if kind == 0:
            ref = a_rows(shift(x, -by), c * chunk, chunk)
        else:
            ref = a_rows(shift(x, 2), c * chunk + direction * half_chunk, half_chunk)
        remote(ref, a_send.at[direction, kind, c], a_recv.at[direction, kind, c], g, shift(x, by)).wait_recv()

    def a_relay(c):
        for direction in (0, 1):
            a_arrived(direction, 0, c)
            launch(a_copy(direction, 1, c))

    n_sent = [0]

    def place(h, first, second):
        return (shift(z, second), shift(y, first)) if h == 0 else (shift(z, first), shift(y, second))

    def device_of(zz, yy, cc):
        return (zz * SIDE + yy) * 2 + cc

    def r_ref(h, at, part):
        start, size = h * half, half
        if part is not None:
            start, size = start + part * quarter, quarter
        return r_rows(at[0], at[1], core, start, size)

    def r_copy(h, at, part, to):
        slot = n_sent[0]
        n_sent[0] += 1
        launch(remote(
            r_ref(h, at, part), r_send.at[slot], r_recv.at[h, at[0] * SIDE + at[1], part or 0],
            device_of(to[0], to[1], core), x,
        ))

    def r_arrived(h, at, part):
        remote(
            r_ref(h, at, part), r_send.at[0], r_recv.at[h, at[0] * SIDE + at[1], part or 0], device_of(z, y, 1 - core), x
        ).wait_recv()

    def to_partner(h, at):
        index = at[0] * SIDE + at[1]
        launch(remote(r_ref(h, at, None), p_send.at[h, index], p_recv.at[h, index], device_of(z, y, 1 - core), x))

    def along_second(h, at):
        for by in (1, -1):
            r_copy(h, at, None, place(h, 0, by))

    own_rot.wait()
    for h in (0, 1):
        at = place(h, 0, 0)
        for by in (1, -1):
            r_copy(h, at, None, place(h, by, 0))
    for c in range(CHUNKS):
        own_coef[c].wait()
        for direction in (0, 1):
            launch(a_copy(direction, 0, c))
    for h in (0, 1):
        at = place(h, 0, 0)
        along_second(h, at)
        to_partner(h, at)
    for direction in (0, 1):
        by = 1 if direction == 0 else -1
        for h in (0, 1):
            at = place(h, -by, 0)
            r_arrived(h, at, None)
            r_copy(h, at, direction, place(h, by, 0))
            along_second(h, at)
            to_partner(h, at)
    for h in (0, 1):
        at = place(h, 2, 0)
        r_arrived(h, at, 0)
        r_arrived(h, at, 1)
        along_second(h, at)
        to_partner(h, at)
    for first in (0, -1, 1, 2):
        for direction in (0, 1):
            by = 1 if direction == 0 else -1
            for h in (0, 1):
                at = place(h, first, -by)
                r_arrived(h, at, None)
                r_copy(h, at, direction, place(h, 0, by))
                to_partner(h, at)
        if first == 0:
            a_relay(0)
        if first == 1:
            a_relay(1)
    for first in (0, -1, 1, 2):
        for h in (0, 1):
            at = place(h, first, 2)
            r_arrived(h, at, 0)
            r_arrived(h, at, 1)
            to_partner(h, at)
    a_relay(2)
    for h in (0, 1):
        def partner_arrived(index, carry):
            zz, yy = index // SIDE, index % SIDE
            remote(
                r_rows(zz, yy, 1 - core, h * half, half), p_send.at[h, index], p_recv.at[h, index],
                device_of(z, y, 1 - core), x,
            ).wait_recv()
            return carry

        lax.fori_loop(0, SIDE * SIDE, partner_arrived, 0)

    def product(block, start, m, j):
        columns = pl.ds(pl.multiple_of(j * TILE_N, TILE_N), TILE_N)
        return columns, jnp.dot(
            a_buf[block, pl.ds(start, m), :], r_buf[block, :, columns], preferred_element_type=jnp.float32
        )

    n_tiles = cols // TILE_N
    m_tiles = rows // TILE_M

    def own_step(step, carry):
        start = pl.multiple_of((step % m_tiles) * TILE_M, 16)
        columns, value = product(x, start, TILE_M, step // m_tiles)
        c_buf[pl.ds(start, TILE_M), columns] = value
        return carry

    lax.fori_loop(0, n_tiles * m_tiles, own_step, 0)
    for c in range(3, CHUNKS):
        a_relay(c)

    def next_step(step, carry):
        start = pl.multiple_of((step % m_tiles) * TILE_M, 16)
        for by in (1, -1):
            columns, value = product(shift(x, by), start, TILE_M, step // m_tiles)
            c_buf[pl.ds(start, TILE_M), columns] += value
        return carry

    lax.fori_loop(0, n_tiles * m_tiles, next_step, 0)
    sq_sum[...] = jnp.zeros_like(sq_sum)
    for c in range(CHUNKS):
        a_arrived(0, 1, c)
        a_arrived(1, 1, c)

        def last_step(j, carry):
            columns, value = product(shift(x, 2), c * chunk, chunk, j)
            total = c_buf[c * chunk:(c + 1) * chunk, columns] + value
            c_buf[c * chunk:(c + 1) * chunk, columns] = total
            sq_sum[:, columns] += jnp.sum(total * total, axis=0, keepdims=True)
            return carry

        lax.fori_loop(0, n_tiles, last_step, 0)

    sq_buf[g] = sq_sum[...]

    def square_copy(source, target, sem):
        return remote(sq_buf.at[source], s_send.at[sem], s_recv.at[source], target, x)

    def send_squares(step, carry):
        square_copy(g, (g + step) % peers, step).start()
        return carry

    def squares_arrived(step, carry):
        source = (g + step) % peers
        square_copy(source, source, step).wait_recv()
        return carry

    def squares_sent(step, carry):
        square_copy(g, (g + step) % peers, step).wait_send()
        return carry

    lax.fori_loop(1, peers, send_squares, 0)
    for copy in sends:
        copy.wait_send()
    lax.fori_loop(1, peers, squares_sent, 0)
    lax.fori_loop(1, peers, squares_arrived, 0)

    total = sq_buf[0]
    for i in range(1, peers):
        total = total + sq_buf[i]
    rms = jnp.sqrt(total / TOTAL_ROWS + 1e-06)
    rms_out[...] = rms
    sq_sum[...] = 1.0 / rms

    def out_copy(i):
        start = i * chunk
        return pltpu.make_async_copy(a_rows(x, start, chunk), out.at[pl.ds(start, chunk), :], out_sem.at[i])

    for c in range(CHUNKS):
        a_buf[x, c * chunk:(c + 1) * chunk, :] = (
            c_buf[c * chunk:(c + 1) * chunk, :] * sq_sum[...]
        ).astype(jnp.bfloat16)
        out_copy(c).start()
    for c in range(CHUNKS):
        out_copy(c).wait()


def body(coefficients, rotation):
    rows, depth = coefficients.shape
    piece, cols = rotation.shape
    peers = lax.axis_size("ga")
    dma = pltpu.SemaphoreType.DMA
    out, rms = pl.pallas_call(
        kernel,
        out_shape=(
            jax.ShapeDtypeStruct((rows, cols), jnp.bfloat16),
            jax.ShapeDtypeStruct((1, cols), jnp.float32),
        ),
        in_specs=[pl.BlockSpec(memory_space=pl.ANY)] * 2,
        out_specs=(pl.BlockSpec(memory_space=pl.ANY), pl.BlockSpec(memory_space=pltpu.VMEM)),
        scratch_shapes=[
            pltpu.VMEM((SIDE, rows, depth), jnp.bfloat16),
            pltpu.VMEM((SIDE, depth, cols), jnp.bfloat16),
            pltpu.VMEM((rows, cols), jnp.float32),
            pltpu.VMEM((1, cols), jnp.float32),
            pltpu.VMEM((peers, 1, cols), jnp.float32),
            dma((CHUNKS + 1,)),
            dma((2, 2, CHUNKS)),
            dma((2, 2, CHUNKS)),
            dma((40,)),
            dma((2, 16, 2)),
            dma((2, 16)),
            dma((2, 16)),
            dma((peers,)),
            dma((peers,)),
            dma((CHUNKS,)),
        ],
        compiler_params=pltpu.CompilerParams(
            collective_id=0, has_side_effects=True, vmem_limit_bytes=64 * 1024 * 1024 - 65536
        ),
        cost_estimate=pl.CostEstimate(
            flops=2 * rows * depth * SIDE * cols, bytes_accessed=4 * rows * depth, transcendentals=0
        ),
    )(coefficients, rotation)
    return out, rms.reshape(cols)


def solution(mesh):
    return jax.shard_map(
        body, mesh=mesh, in_specs=(P("ga", "ba"), P("ga", "ba")), out_specs=(P("ga", "ba"), P("ba")), check_vma=False
    )
```

time: 260 us -> 156 us (0.60)
  blocking collectives: 195 us -> 0 us
  Pallas kernels: 0 us -> 149 us
  matrix products: 34 us -> 0 us
  between operations: 14 us -> 0.64 us
  local copies, waits for them, and re-layouts: 10.1 us -> 4.29 us
  other arithmetic: 6.32 us -> 1.31 us
    all_to_all x2 -> x0, blocking collectives: 195 us -> none  [copy_for_each(): return lax.all_to_all(copies, axis, split_axis=0, concat_axis=0, tiled=True)]
    pallas_call x0 -> x1, Pallas kernels: none -> 149 us  [body(): pl.pallas_call(kernel, out_shape=(jax.ShapeDtypeStruct((rows, cols), jnp....]
    dot_general x1 -> x0, matrix products: 34 us -> none  [body(): jnp.dot(gather_directly(coefficients, 'ba', 1), column_block, preferred_e...]
    convert_element_type x1 -> x0, other arithmetic: 6.18 us -> none  [body(): return ((rotated / band_rms).astype(jnp.bfloat16), band_rms)]
    broadcast_in_dim x2 -> x0, local copies, waits for them, and re-layouts: 3.87 us -> none  [copy_for_each(): copies = jnp.broadcast_to(array, (lax.axis_size(axis), *array.shape))]
    unnamed x3 -> x1, local copies, waits for them, and re-layouts: 6.27 us -> 4.29 us
  transfers between devices with their start and end apart: 1 -> 0, of which waited for: 0 -> 0; matrix products, arithmetic and copies ran while one was open for 4% -> 0% of each run, Pallas kernels for 0% -> 0%
where the time goes in v1:
time: 156 us
  Pallas kernels  149 us (96%)
  local copies, waits for them, and re-layouts  4.29 us (3%)
    pallas_call x1, Pallas kernels, body(): pl.pallas_call(kernel, out_shape=(jax.ShapeDtypeStruct((rows, cols), jnp....  149 us
    unnamed x1, local copies, waits for them, and re-layouts  4.29 us

profile of v1, /device:TPU:1, one launch (start us, length us, event | category | flops | bytes accessed | tf_op | source)
XLA Modules:
  0.0 155.6 jit_solution(4704138177055863320)
XLA Ops:
  0.6 149.4 %shard_map.41 = (bf16[1280,1536]{1,0:T(8,128)(2,1)}, f32[1,1536]{1,0:T(1,128)}) custom-call(bf16[1280,1536]{1,0:T(8,128)(2,1)} %coef.1, bf16[192,1536]{1,0:T(8,128)(2,1)} %rot.1), custom_call_target="tpu_custom_call" | custom-call | flops 24159191040 | bytes 7864320 | tf_op jit(solution)/shard_map/pallas_call | solution.py:284
  150.0 1.3 reduce
  151.3 4.3 %copy.5 = bf16[1280,1536]{1,0:T(8,128)(2,1)} copy(bf16[1280,1536]{1,0:T(8,128)(2,1)} %get-tuple-element.8) | data formatting | bytes 7864320

commit v2 on v1

--- a/solution.py
+++ b/solution.py
@@ -9,21 +9,21 @@
 
 MESH = pl.DeviceIdType.MESH
 SIDE = 4
+SIZES = (192, 192, 192, 192, 192, 192, 64, 64)
 CHUNKS = 8
 TILE_M = 320
 TILE_N = 512
 TOTAL_ROWS = 40960
 
 
-def kernel(
-    coef, rot, out, rms_out, a_buf, r_buf, c_buf, sq_sum, sq_buf,
-    load_sem, a_send, a_recv, r_send, r_recv, p_send, p_recv, s_send, s_recv, out_sem,
+def gather_multiply(
+    coef, rot, c_buf, sq_buf, a_buf, r_buf, sq_sum,
+    load_sem, a_send, a_recv, r_send, r_recv, p_send, p_recv, s_send, s_recv,
 ):
     rows, depth = coef.shape
     piece, cols = rot.shape
     peers = 2 * SIDE * SIDE
-    chunk = rows // CHUNKS
-    half_chunk = chunk // 2
+    starts = [sum(SIZES[:c]) for c in range(len(SIZES))]
     half = piece // 2
     quarter = half // 2
 
@@ -37,36 +37,32 @@
     def shift(value, by):
         return (value + by + SIDE) % SIDE
 
+    def device_of(zz, yy, cc):
+        return (zz * SIDE + yy) * 2 + cc
+
     def a_rows(block, start, size):
         return a_buf.at[block, pl.ds(start, size), :]
 
     def r_rows(zz, yy, cc, start, size):
         return r_buf.at[zz, pl.ds(pl.multiple_of((yy * 2 + cc) * piece + start, 16), size), :]
 
-    own_rot = pltpu.make_async_copy(rot, r_rows(z, y, core, 0, piece), load_sem.at[CHUNKS])
+    own_rot = pltpu.make_async_copy(rot, r_rows(z, y, core, 0, piece), load_sem.at[len(SIZES)])
     own_rot.start()
     own_coef = []
-    for c in range(CHUNKS):
-        copy = pltpu.make_async_copy(
-            coef.at[pl.ds(c * chunk, chunk), :], a_rows(x, c * chunk, chunk), load_sem.at[c]
-        )
+    for c, (start, size) in enumerate(zip(starts, SIZES)):
+        copy = pltpu.make_async_copy(coef.at[pl.ds(start, size), :], a_rows(x, start, size), load_sem.at[c])
         copy.start()
         own_coef.append(copy)
 
     barrier = pltpu.get_barrier_semaphore()
 
-    def greet(step, carry):
-        pl.semaphore_signal(
-            barrier, inc=1, device_id={"ga": (g + step) % peers, "ba": x}, device_id_type=MESH
-        )
-        return carry
-
-    lax.fori_loop(1, peers, greet, 0)
-    for by in (1, -1):
-        pl.semaphore_signal(
-            barrier, inc=1, device_id={"ga": g, "ba": shift(x, by)}, device_id_type=MESH
-        )
-    pl.semaphore_wait(barrier, peers + 1)
+    near = [(device_of(shift(z, by), y, core), x) for by in (1, -1)]
+    near += [(device_of(z, shift(y, by), core), x) for by in (1, -1)]
+    near += [(g, shift(x, by)) for by in (1, -1)]
+    near += [(device_of(z, y, 1 - core), x)]
+    for ga, ba in near:
+        pl.semaphore_signal(barrier, inc=1, device_id={"ga": ga, "ba": ba}, device_id_type=MESH)
+    pl.semaphore_wait(barrier, len(near))
 
     def remote(ref, send, recv, ga, ba):
         return pltpu.make_async_remote_copy(
@@ -81,17 +77,17 @@
     def a_copy(direction, kind, c):
         by = 1 if direction == 0 else -1
         if kind == 0:
-            ref = a_rows(x, c * chunk, chunk)
+            ref = a_rows(x, starts[c], SIZES[c])
         else:
-            ref = a_rows(shift(x, -by), c * chunk + direction * half_chunk, half_chunk)
+            ref = a_rows(shift(x, -by), starts[c] + direction * (SIZES[c] // 2), SIZES[c] // 2)
         return remote(ref, a_send.at[direction, kind, c], a_recv.at[direction, kind, c], g, shift(x, by))
 
     def a_arrived(direction, kind, c):
         by = 1 if direction == 0 else -1
         if kind == 0:
-            ref = a_rows(shift(x, -by), c * chunk, chunk)
+            ref = a_rows(shift(x, -by), starts[c], SIZES[c])
         else:
-            ref = a_rows(shift(x, 2), c * chunk + direction * half_chunk, half_chunk)
+            ref = a_rows(shift(x, 2), starts[c] + direction * (SIZES[c] // 2), SIZES[c] // 2)
         remote(ref, a_send.at[direction, kind, c], a_recv.at[direction, kind, c], g, shift(x, by)).wait_recv()
 
     def a_relay(c):
@@ -103,9 +99,6 @@
 
     def place(h, first, second):
         return (shift(z, second), shift(y, first)) if h == 0 else (shift(z, first), shift(y, second))
-
-    def device_of(zz, yy, cc):
-        return (zz * SIDE + yy) * 2 + cc
 
     def r_ref(h, at, part):
         start, size = h * half, half
@@ -139,7 +132,7 @@
         at = place(h, 0, 0)
         for by in (1, -1):
             r_copy(h, at, None, place(h, by, 0))
-    for c in range(CHUNKS):
+    for c in range(len(SIZES)):
         own_coef[c].wait()
         for direction in (0, 1):
             launch(a_copy(direction, 0, c))
@@ -207,7 +200,7 @@
         return carry
 
     lax.fori_loop(0, n_tiles * m_tiles, own_step, 0)
-    for c in range(3, CHUNKS):
+    for c in range(3, len(SIZES)):
         a_relay(c)
 
     def next_step(step, carry):
@@ -219,14 +212,14 @@
 
     lax.fori_loop(0, n_tiles * m_tiles, next_step, 0)
     sq_sum[...] = jnp.zeros_like(sq_sum)
-    for c in range(CHUNKS):
+    for c in range(len(SIZES)):
         a_arrived(0, 1, c)
         a_arrived(1, 1, c)
 
         def last_step(j, carry):
-            columns, value = product(shift(x, 2), c * chunk, chunk, j)
-            total = c_buf[c * chunk:(c + 1) * chunk, columns] + value
-            c_buf[c * chunk:(c + 1) * chunk, columns] = total
+            columns, value = product(shift(x, 2), starts[c], SIZES[c], j)
+            total = c_buf[starts[c]:starts[c] + SIZES[c], columns] + value
+            c_buf[starts[c]:starts[c] + SIZES[c], columns] = total
             sq_sum[:, columns] += jnp.sum(total * total, axis=0, keepdims=True)
             return carry
 
@@ -256,21 +249,24 @@
     lax.fori_loop(1, peers, squares_sent, 0)
     lax.fori_loop(1, peers, squares_arrived, 0)
 
+
+def normalize(c_buf, sq_buf, out, rms_out, scale, staged, out_sem):
+    rows, cols = c_buf.shape
+    chunk = rows // CHUNKS
     total = sq_buf[0]
-    for i in range(1, peers):
+    for i in range(1, sq_buf.shape[0]):
         total = total + sq_buf[i]
     rms = jnp.sqrt(total / TOTAL_ROWS + 1e-06)
-    rms_out[...] = rms
-    sq_sum[...] = 1.0 / rms
-
-    def out_copy(i):
-        start = i * chunk
-        return pltpu.make_async_copy(a_rows(x, start, chunk), out.at[pl.ds(start, chunk), :], out_sem.at[i])
+    rms_out[...] = rms.reshape(cols)
+    scale[...] = 1.0 / rms
+
+    def out_copy(c):
+        part = pl.ds(c * chunk, chunk)
+        return pltpu.make_async_copy(staged.at[part, :], out.at[part, :], out_sem.at[c])
 
     for c in range(CHUNKS):
-        a_buf[x, c * chunk:(c + 1) * chunk, :] = (
-            c_buf[c * chunk:(c + 1) * chunk, :] * sq_sum[...]
-        ).astype(jnp.bfloat16)
+        part = pl.ds(c * chunk, chunk)
+        staged[part, :] = (c_buf[part, :] * scale[...]).astype(jnp.bfloat16)
         out_copy(c).start()
     for c in range(CHUNKS):
         out_copy(c).wait()
@@ -281,39 +277,48 @@
     piece, cols = rotation.shape
     peers = lax.axis_size("ga")
     dma = pltpu.SemaphoreType.DMA
-    out, rms = pl.pallas_call(
-        kernel,
-        out_shape=(
-            jax.ShapeDtypeStruct((rows, cols), jnp.bfloat16),
-            jax.ShapeDtypeStruct((1, cols), jnp.float32),
-        ),
+    rotated, squares = pl.pallas_call(
+        gather_multiply,
+        out_shape=(pltpu.VMEM((rows, cols), jnp.float32), pltpu.VMEM((peers, 1, cols), jnp.float32)),
         in_specs=[pl.BlockSpec(memory_space=pl.ANY)] * 2,
-        out_specs=(pl.BlockSpec(memory_space=pl.ANY), pl.BlockSpec(memory_space=pltpu.VMEM)),
+        out_specs=(pl.BlockSpec(memory_space=pltpu.VMEM), pl.BlockSpec(memory_space=pltpu.VMEM)),
         scratch_shapes=[
             pltpu.VMEM((SIDE, rows, depth), jnp.bfloat16),
             pltpu.VMEM((SIDE, depth, cols), jnp.bfloat16),
-            pltpu.VMEM((rows, cols), jnp.float32),
             pltpu.VMEM((1, cols), jnp.float32),
-            pltpu.VMEM((peers, 1, cols), jnp.float32),
-            dma((CHUNKS + 1,)),
-            dma((2, 2, CHUNKS)),
-            dma((2, 2, CHUNKS)),
+            dma((len(SIZES) + 1,)),
+            dma((2, 2, len(SIZES))),
+            dma((2, 2, len(SIZES))),
             dma((40,)),
             dma((2, 16, 2)),
             dma((2, 16)),
             dma((2, 16)),
             dma((peers,)),
             dma((peers,)),
-            dma((CHUNKS,)),
         ],
         compiler_params=pltpu.CompilerParams(
-            collective_id=0, has_side_effects=True, vmem_limit_bytes=64 * 1024 * 1024 - 65536
+            collective_id=0, has_side_effects=True, vmem_limit_bytes=50 * 1024 * 1024
         ),
         cost_estimate=pl.CostEstimate(
             flops=2 * rows * depth * SIDE * cols, bytes_accessed=4 * rows * depth, transcendentals=0
         ),
     )(coefficients, rotation)
-    return out, rms.reshape(cols)
+    return pl.pallas_call(
+        normalize,
+        out_shape=(
+            jax.ShapeDtypeStruct((rows, cols), jnp.bfloat16),
+            jax.ShapeDtypeStruct((cols,), jnp.float32),
+        ),
+        in_specs=[pl.BlockSpec(memory_space=pltpu.VMEM)] * 2,
+        out_specs=(pl.BlockSpec(memory_space=pl.ANY), pl.BlockSpec(memory_space=pltpu.VMEM)),
+        scratch_shapes=[
+            pltpu.VMEM((1, cols), jnp.float32),
+            pltpu.VMEM((rows, cols), jnp.bfloat16),
+            dma((CHUNKS,)),
+        ],
+        compiler_params=pltpu.CompilerParams(vmem_limit_bytes=20 * 1024 * 1024),
+        cost_estimate=pl.CostEstimate(flops=rows * cols, bytes_accessed=6 * rows * cols, transcendentals=0),
+    )(rotated, squares)
 
 
 def solution(mesh):

time: 156 us -> 149 us (0.955)
  local copies, waits for them, and re-layouts: 4.29 us -> 0 us
    unnamed x1 -> x0, local copies, waits for them, and re-layouts: 4.29 us -> none
    pallas_call x1 -> x2, Pallas kernels: 149 us -> 148 us  [the longest x1 145 us: body(): pl.pallas_call(gather_multiply, out_shape=(pltpu.VMEM((rows, cols), jnp.f...]
where the time goes in v2:
time: 149 us; the launch traced here: 148 us
  Pallas kernels  148 us (99%)
    pallas_call x1, Pallas kernels, body(): pl.pallas_call(gather_multiply, out_shape=(pltpu.VMEM((rows, cols), jnp.f...  145 us

profile of v2, /device:TPU:1, one launch (start us, length us, event | category | flops | bytes accessed | tf_op | source)
XLA Modules:
  0.0 148.5 jit_solution(2670242685183202726)
XLA Ops:
  0.6 145.1 %shard_map.41 = (f32[1280,1536]{1,0:T(8,128)S(1)}, f32[32,1,1536]{2,1,0:T(1,128)S(1)}) custom-call(bf16[1280,1536]{1,0:T(8,128)(2,1)} %coef.1, bf16[192,1536]{1,0:T(8,128)(2,1)} %rot.1), custom_call_target="tpu_custom_call" | custom-call | flops 24159191040 | bytes 7864320 | tf_op jit(solution)/shard_map/pallas_call | solution.py:280
  145.7 2.7 %shard_map.42 = (bf16[1280,1536]{1,0:T(8,128)(2,1)}, f32[1536]{0:T(1024)}) custom-call(f32[1280,1536]{1,0:T(8,128)S(1)} %get-tuple-element.4.c_buf, f32[32,1,1536]{2,1,0:T(1,128)S(1)} %get-tuple-element.5.sq_buf), custom_call_target="tpu_custom_call" | custom-call | flops 1966080 | bytes 11796480 | tf_op jit(solution)/shard_map/pallas_call | solution.py:306

commit v3 on v2

v3 whole, which is shorter than its diff:
```python
import functools

import jax
import jax.numpy as jnp
from jax import lax
from jax.experimental import pallas as pl
from jax.experimental.pallas import tpu as pltpu
from jax.sharding import PartitionSpec as P

MESH = pl.DeviceIdType.MESH
SIDE = 4
SIZES = (256, 256, 256, 256, 192, 64)
CHUNKS = 8
TILE_M = 320
TILE_N = 512
TOTAL_ROWS = 40960


def gather_multiply(
    coef, rot, c_buf, sq_buf, a_buf, r_buf, sq_sum,
    load_sem, a_sem, relay_sem, r_sem, sem,
):
    rows, depth = coef.shape
    piece, cols = rot.shape
    peers = 2 * SIDE * SIDE
    starts = [sum(SIZES[:c]) for c in range(len(SIZES))]
    half = piece // 2
    quarter = half // 2

    g = lax.axis_index("ga")
    x = lax.axis_index("ba")
    core = g % 2
    y = (g // 2) % SIDE
    z = g // (2 * SIDE)
    a_send, r_send, p_send, p_recv, s_send, s_recv = (sem.at[i] for i in range(6))

    def shift(value, by):
        return (value + by + SIDE) % SIDE

    def device_of(zz, yy, cc):
        return (zz * SIDE + yy) * 2 + cc

    def a_rows(block, start, size):
        return a_buf.at[block, pl.ds(start, size), :]

    def r_rows(zz, yy, cc, start, size):
        return r_buf.at[pl.ds(pl.multiple_of(device_of(zz, yy, cc) * piece + start, 16), size), :]

    own_rot = pltpu.make_async_copy(rot, r_rows(z, y, core, 0, piece), load_sem.at[1])
    own_rot.start()
    own_coef = pltpu.make_async_copy(coef, a_buf.at[x], load_sem.at[0])
    own_coef.start()

    barrier = pltpu.get_barrier_semaphore()

    near = [(device_of(shift(z, by), y, core), x) for by in (1, -1)]
    near += [(device_of(z, shift(y, by), core), x) for by in (1, -1)]
    near += [(g, shift(x, by)) for by in (1, -1)]
    near += [(device_of(z, y, 1 - core), x)]
    for ga, ba in near:
        pl.semaphore_signal(barrier, inc=1, device_id={"ga": ga, "ba": ba}, device_id_type=MESH)
    pl.semaphore_wait(barrier, len(near))

    def remote(ref, send, recv, ga, ba):
        return pltpu.make_async_remote_copy(
            src_ref=ref, dst_ref=ref, send_sem=send, recv_sem=recv,
            device_id={"ga": ga, "ba": ba}, device_id_type=MESH,
        )

    def half_rows(block, direction, c):
        return a_rows(block, starts[c] + direction * (SIZES[c] // 2), SIZES[c] // 2)

    def a_start(direction, c):
        to = shift(x, 1 - 2 * direction)
        remote(a_rows(x, starts[c], SIZES[c]), a_send, a_sem.at[direction, c], g, to).start()

    def a_wait(direction, c):
        origin = shift(x, 2 * direction - 1)
        remote(a_rows(origin, starts[c], SIZES[c]), a_send, a_sem.at[direction, c], g, origin).wait_recv()

    def relay_start(direction, c):
        origin, to = shift(x, 2 * direction - 1), shift(x, 1 - 2 * direction)
        remote(half_rows(origin, direction, c), a_send, relay_sem.at[c], g, to).start()

    def relay_wait(c):
        origin = shift(x, 2)
        remote(a_rows(origin, starts[c], SIZES[c]), a_send, relay_sem.at[c], g, shift(x, 1)).wait_recv()

    def a_relay(c):
        for direction in (0, 1):
            a_wait(direction, c)
            relay_start(direction, c)

    def place(h, first, second):
        return (shift(z, second), shift(y, first)) if h == 0 else (shift(z, first), shift(y, second))

    def r_ref(h, at, part):
        if part is None:
            return r_rows(at[0], at[1], core, h * half, half)
        return r_rows(at[0], at[1], core, h * half + part * quarter, quarter)

    def r_start(h, at, part, slot, to):
        remote(r_ref(h, at, part), r_send, r_sem.at[h, slot], device_of(to[0], to[1], core), x).start()

    def r_wait(h, at, slot):
        remote(r_ref(h, at, None), r_send, r_sem.at[h, slot], device_of(z, y, 1 - core), x).wait_recv()

    def to_partner(h, at):
        remote(r_ref(h, at, None), p_send, p_recv, device_of(z, y, 1 - core), x).start()

    places = {0: 0, -1: 1, 1: 2, 2: 3}

    def slot_of(first, kind):
        return 3 + 3 * places[first] + kind

    def along_second(h, at, first):
        for direction in (0, 1):
            r_start(h, at, None, slot_of(first, direction), place(h, 0, 1 - 2 * direction))

    own_rot.wait()
    for h in (0, 1):
        for direction in (0, 1):
            r_start(h, (z, y), None, direction, place(h, 1 - 2 * direction, 0))
    own_coef.wait()
    for c in range(len(SIZES)):
        for direction in (0, 1):
            a_start(direction, c)
    for h in (0, 1):
        along_second(h, (z, y), 0)
        to_partner(h, (z, y))
    for direction in (0, 1):
        by = 1 - 2 * direction
        for h in (0, 1):
            at = place(h, -by, 0)
            r_wait(h, at, direction)
            r_start(h, at, direction, 2, place(h, by, 0))
            along_second(h, at, -by)
            to_partner(h, at)
    for h in (0, 1):
        at = place(h, 2, 0)
        r_wait(h, at, 2)
        along_second(h, at, 2)
        to_partner(h, at)
    for first in (0, -1, 1, 2):
        for direction in (0, 1):
            by = 1 - 2 * direction
            for h in (0, 1):
                at = place(h, first, -by)
                r_wait(h, at, slot_of(first, direction))
                r_start(h, at, direction, slot_of(first, 2), place(h, 0, by))
                to_partner(h, at)
        if first == 0:
            a_relay(0)
    for first in (0, -1, 1, 2):
        for h in (0, 1):
            at = place(h, first, 2)
            r_wait(h, at, slot_of(first, 2))
            to_partner(h, at)
    a_relay(1)
    pieces = SIDE * SIDE * piece
    remote(r_buf.at[pl.ds(0, pieces), :], p_send, p_recv, device_of(z, y, 1 - core), x).wait()

    def product(block, start, m, j):
        columns = pl.ds(pl.multiple_of(j * TILE_N, TILE_N), TILE_N)
        return columns, jnp.dot(
            a_buf[block, pl.ds(start, m), :], r_buf[pl.ds(pl.multiple_of(block * depth, depth), depth), columns], preferred_element_type=jnp.float32
        )

    n_tiles = cols // TILE_N
    m_tiles = rows // TILE_M

    def own_step(step, carry):
        start = pl.multiple_of((step % m_tiles) * TILE_M, 16)
        columns, value = product(x, start, TILE_M, step // m_tiles)
        c_buf[pl.ds(start, TILE_M), columns] = value
        return carry

    lax.fori_loop(0, n_tiles * m_tiles, own_step, 0)
    for c in range(2, len(SIZES)):
        a_relay(c)

    def next_step(step, carry):
        start = pl.multiple_of((step % m_tiles) * TILE_M, 16)
        for by in (1, -1):
            columns, value = product(shift(x, by), start, TILE_M, step // m_tiles)
            c_buf[pl.ds(start, TILE_M), columns] += value
        return carry

    lax.fori_loop(0, n_tiles * m_tiles, next_step, 0)
    sq_sum[...] = jnp.zeros_like(sq_sum)
    for c in range(len(SIZES)):
        relay_wait(c)

        def last_step(j, carry):
            columns, value = product(shift(x, 2), starts[c], SIZES[c], j)
            total = c_buf[starts[c]:starts[c] + SIZES[c], columns] + value
            c_buf[starts[c]:starts[c] + SIZES[c], columns] = total
            sq_sum[:, columns] += jnp.sum(total * total, axis=0, keepdims=True)
            return carry

        lax.fori_loop(0, n_tiles, last_step, 0)

    sq_buf[g] = sq_sum[...]
    others = [(dz, dy, dc) for dz in range(-1, 3) for dy in range(-1, 3) for dc in (0, 1) if (dz, dy, dc) != (0, 0, 0)]
    for dz, dy, dc in sorted(others, key=lambda by: -(abs(by[0]) + abs(by[1]))):
        peer = device_of(shift(z, dz), shift(y, dy), (core + dc) % 2)
        remote(sq_buf.at[g], s_send, s_recv, peer, x).start()
    remote(a_buf.at[pl.ds(0, 3)], a_send, a_sem.at[0, 0], g, shift(x, 1)).wait_send()
    sent = 15 * piece
    remote(r_buf.at[pl.ds(0, sent), :], r_send, r_sem.at[0, 0], device_of(z, y, 1 - core), x).wait_send()
    remote(sq_buf.at[pl.ds(0, peers - 1)], s_send, s_recv, device_of(z, y, 1 - core), x).wait()


def normalize(c_buf, sq_buf, out, rms_out, scale, staged, out_sem):
    rows, cols = c_buf.shape
    chunk = rows // CHUNKS
    total = sq_buf[0]
    for i in range(1, sq_buf.shape[0]):
        total = total + sq_buf[i]
    rms = jnp.sqrt(total / TOTAL_ROWS + 1e-06)
    rms_out[...] = rms.reshape(cols)
    scale[...] = 1.0 / rms

    def out_copy(c):
        part = pl.ds(c * chunk, chunk)
        return pltpu.make_async_copy(staged.at[part, :], out.at[part, :], out_sem.at[c])

    for c in range(CHUNKS):
        part = pl.ds(c * chunk, chunk)
        staged[part, :] = (c_buf[part, :] * scale[...]).astype(jnp.bfloat16)
        out_copy(c).start()
    for c in range(CHUNKS):
        out_copy(c).wait()


def body(coefficients, rotation):
    rows, depth = coefficients.shape
    piece, cols = rotation.shape
    peers = lax.axis_size("ga")
    dma = pltpu.SemaphoreType.DMA
    rotated, squares = pl.pallas_call(
        gather_multiply,
        out_shape=(pltpu.VMEM((rows, cols), jnp.float32), pltpu.VMEM((peers, 1, cols), jnp.float32)),
        in_specs=[pl.BlockSpec(memory_space=pl.ANY)] * 2,
        out_specs=(pl.BlockSpec(memory_space=pltpu.VMEM), pl.BlockSpec(memory_space=pltpu.VMEM)),
        scratch_shapes=[
            pltpu.VMEM((SIDE, rows, depth), jnp.bfloat16),
            pltpu.VMEM((SIDE * depth, cols), jnp.bfloat16),
            pltpu.VMEM((1, cols), jnp.float32),
            dma((2,)),
            dma((2, len(SIZES))),
            dma((len(SIZES),)),
            dma((2, 15)),
            dma((6,)),
        ],
        compiler_params=pltpu.CompilerParams(
            collective_id=0, has_side_effects=True, vmem_limit_bytes=50 * 1024 * 1024
        ),
        cost_estimate=pl.CostEstimate(
            flops=2 * rows * depth * SIDE * cols, bytes_accessed=4 * rows * depth, transcendentals=0
        ),
    )(coefficients, rotation)
    return pl.pallas_call(
        normalize,
        out_shape=(
            jax.ShapeDtypeStruct((rows, cols), jnp.bfloat16),
            jax.ShapeDtypeStruct((cols,), jnp.float32),
        ),
        in_specs=[pl.BlockSpec(memory_space=pltpu.VMEM)] * 2,
        out_specs=(pl.BlockSpec(memory_space=pl.ANY), pl.BlockSpec(memory_space=pltpu.VMEM)),
        scratch_shapes=[
            pltpu.VMEM((1, cols), jnp.float32),
            pltpu.VMEM((rows, cols), jnp.bfloat16),
            dma((CHUNKS,)),
        ],
        compiler_params=pltpu.CompilerParams(vmem_limit_bytes=20 * 1024 * 1024),
        cost_estimate=pl.CostEstimate(flops=rows * cols, bytes_accessed=6 * rows * cols, transcendentals=0),
    )(rotated, squares)


def solution(mesh):
    return jax.shard_map(
        body, mesh=mesh, in_specs=(P("ga", "ba"), P("ga", "ba")), out_specs=(P("ga", "ba"), P("ba")), check_vma=False
    )
```

time: 149 us -> 148 us (level)
  no operation moved by 1% of the time
where the time goes in v3:
time: 148 us; the launch traced here: 147 us
  Pallas kernels  147 us (99%)
    pallas_call x1, Pallas kernels, body(): pl.pallas_call(gather_multiply, out_shape=(pltpu.VMEM((rows, cols), jnp.f...  144 us

profile of v3, /device:TPU:1, one launch (start us, length us, event | category | flops | bytes accessed | tf_op | source)
XLA Modules:
  0.0 147.4 jit_solution(4875985506020221795)
XLA Ops:
  0.6 144.0 %shard_map.41 = (f32[1280,1536]{1,0:T(8,128)S(1)}, f32[32,1,1536]{2,1,0:T(1,128)S(1)}) custom-call(bf16[1280,1536]{1,0:T(8,128)(2,1)} %coef.1, bf16[192,1536]{1,0:T(8,128)(2,1)} %rot.1), custom_call_target="tpu_custom_call" | custom-call | flops 24159191040 | bytes 7864320 | tf_op jit(solution)/shard_map/pallas_call | solution.py:241
  144.7 2.7 %shard_map.42 = (bf16[1280,1536]{1,0:T(8,128)(2,1)}, f32[1536]{0:T(1024)}) custom-call(f32[1280,1536]{1,0:T(8,128)S(1)} %get-tuple-element.4.c_buf, f32[32,1,1536]{2,1,0:T(1,128)S(1)} %get-tuple-element.5.sq_buf), custom_call_target="tpu_custom_call" | custom-call | flops 1966080 | bytes 11796480 | tf_op jit(solution)/shard_map/pallas_call | solution.py:263

commit v4 on v3

v4 whole, which is shorter than its diff:
```python
import jax
import jax.numpy as jnp
from jax import lax
from jax.experimental import pallas as pl
from jax.experimental.pallas import tpu as pltpu
from jax.sharding import PartitionSpec as P

MESH = pl.DeviceIdType.MESH
SIDE = 4
LAST = (256, 64)
CHUNKS = 8
TILE_N = 512
TOTAL_ROWS = 40960
SENDS = ("a_send", "r_send", "s_send", "p_send", "x_send", "e_send", "q_send", "t_send")
ARRIVALS = ("x_recv", "e_recv", "q_recv", "t_recv", "p_recv", "p_recv00", "p_recv01", "p_recv10", "p_recv11")
SEMS = {name: i for i, name in enumerate(SENDS + ARRIVALS)}


def gather_multiply(
    coef, rot, c_buf, sq_buf, a_buf, r_buf, r2_buf, ext, sq_sum, sq_out, sq_in,
    load_sem, a_sem, relay_sem, last_sem, r_sem, r2_sem, sems,
):
    rows, depth = coef.shape
    piece, cols = rot.shape
    peers = 2 * SIDE * SIDE
    quarter = rows // SIDE
    side_cols = cols // 2
    k_all = peers * piece
    chip = 2 * piece

    g = lax.axis_index("ga")
    x = lax.axis_index("ba")
    core = g % 2
    y = (g // 2) % SIDE
    z = g // (2 * SIDE)
    sem = {name: sems.at[i] for name, i in SEMS.items()}

    def shift(value, by):
        return (value + by + SIDE) % SIDE

    def device_of(zz, yy, cc):
        return (zz * SIDE + yy) * 2 + cc

    partner = device_of(z, y, 1 - core)

    def rows_at(start, size, align=16):
        return pl.ds(pl.multiple_of(start, align), size)

    def a_part(block, by, start=0, size=None):
        at = block * rows + shift(x, by) * quarter + start
        return rows_at(at, quarter if size is None else size, 32)

    def piece_rows(at, cc, start=0, size=None):
        return rows_at(device_of(at[0], at[1], cc) * piece + start, piece if size is None else size)

    own = (z, y)

    own_rot = pltpu.make_async_copy(rot, r_buf.at[piece_rows(own, core), :], load_sem.at[1])
    own_rot.start()
    own_coef = pltpu.make_async_copy(coef, a_buf.at[rows_at(x * rows, rows), :], load_sem.at[0])
    own_coef.start()

    barrier = pltpu.get_barrier_semaphore()
    near = [(device_of(shift(z, by), y, core), x) for by in (1, -1)]
    near += [(device_of(z, shift(y, by), core), x) for by in (1, -1)]
    near += [(g, shift(x, by)) for by in (1, -1)]
    near += [(partner, x)]
    for ga, ba in near:
        pl.semaphore_signal(barrier, inc=1, device_id={"ga": ga, "ba": ba}, device_id_type=MESH)
    pl.semaphore_wait(barrier, len(near))

    def remote(src, dst, send, recv, ga, ba):
        return pltpu.make_async_remote_copy(
            src_ref=src, dst_ref=dst, send_sem=send, recv_sem=recv,
            device_id={"ga": ga, "ba": ba}, device_id_type=MESH,
        )

    order = lambda by: (by, 2, 0)

    def a_move(part, recv, to):
        ref = a_buf.at[part, :]
        return remote(ref, ref, sem["a_send"], recv, g, to)

    def a_start(direction, i):
        by = 1 - 2 * direction
        a_move(a_part(x, order(by)[i]), a_sem.at[direction, i], shift(x, by)).start()

    def a_wait(direction, i):
        by = 1 - 2 * direction
        a_move(a_part(shift(x, -by), order(by)[i] - by), a_sem.at[direction, i], shift(x, by)).wait_recv()

    def relay_start(direction):
        by = 1 - 2 * direction
        a_move(a_part(shift(x, -by), 0), relay_sem.at[direction], shift(x, by)).start()

    def relay_wait(direction):
        by = 1 - 2 * direction
        a_move(a_part(shift(x, 2), -by), relay_sem.at[direction], shift(x, by)).wait_recv()

    last_starts = [sum(LAST[:c]) for c in range(len(LAST))]

    def last_start(direction, c):
        by = 1 - 2 * direction
        size = LAST[c] // 2
        part = a_part(shift(x, -by), by, last_starts[c] + direction * size, size)
        a_move(part, last_sem.at[c], shift(x, by)).start()

    def last_wait(c):
        a_move(a_part(shift(x, 2), 0, last_starts[c], LAST[c]), last_sem.at[c], shift(x, 1)).wait_recv()

    def place(h, first, second):
        return (shift(z, second), shift(y, first)) if h == 0 else (shift(z, first), shift(y, second))

    def r_ref(q, h, at, part, cc):
        if q == 0:
            size = piece // 2
            start = h * size
            ref = r_buf
            if part is not None:
                size = size // 2
                start = start + part * size
            return ref.at[piece_rows(at, cc, start, size), :]
        size, start = piece, h * k_all
        if part is not None:
            size = size // 2
            start = start + part * size
        return r2_buf.at[piece_rows(at, cc, start, size), :]

    def r_start(q, h, at, part, slot, to):
        ref = r_ref(q, h, at, part, core)
        recv = (r_sem if q == 0 else r2_sem).at[h, slot]
        remote(ref, ref, sem["r_send"] if q == 0 else sem["s_send"], recv, device_of(to[0], to[1], core), x).start()

    def r_wait(q, h, at, slot):
        ref = r_ref(q, h, at, None, core)
        recv = (r_sem if q == 0 else r2_sem).at[h, slot]
        remote(ref, ref, sem["r_send"], recv, partner, x).wait_recv()

    def to_partner(q, h, at, late):
        ref = r_ref(q, h, at, None, core)
        recv = sem["p_recv"] if q == 0 else sem["p_recv%d%d" % (h, late)]
        remote(ref, ref, sem["p_send"] if q == 0 else sem["t_send"], recv, partner, x).start()

    places = {0: 0, -1: 1, 1: 2, 2: 3}

    def slot_of(first, kind):
        return 3 + 3 * places[first] + kind

    def late_of(first):
        return 0

    def along_second(q, h, at, first):
        for direction in (0, 1):
            r_start(q, h, at, None, slot_of(first, direction), place(h, 0, 1 - 2 * direction))

    def r_own_first(q):
        for h in (0, 1):
            for direction in (0, 1):
                r_start(q, h, own, None, direction, place(h, 1 - 2 * direction, 0))

    def r_own_second(q):
        for h in (0, 1):
            along_second(q, h, own, 0)
            to_partner(q, h, own, 0)

    def r_first(q, direction, h):
        by = 1 - 2 * direction
        at = place(h, -by, 0)
        r_wait(q, h, at, direction)
        r_start(q, h, at, direction, 2, place(h, by, 0))
        along_second(q, h, at, -by)
        to_partner(q, h, at, 0)

    def r_opposite(q, h):
        at = place(h, 2, 0)
        r_wait(q, h, at, 2)
        along_second(q, h, at, 2)
        to_partner(q, h, at, 0)

    def r_second(q, first, direction, h):
        by = 1 - 2 * direction
        at = place(h, first, -by)
        r_wait(q, h, at, slot_of(first, direction))
        r_start(q, h, at, direction, slot_of(first, 2), place(h, 0, by))
        to_partner(q, h, at, 0)

    def r_second_opposite(q, first, h):
        at = place(h, first, 2)
        r_wait(q, h, at, slot_of(first, 2))
        to_partner(q, h, at, 1)

    FIRSTS = (0, -1, 1, 2)

    def product(k, by, start, size, columns):
        return jnp.dot(
            a_buf[a_part(shift(x, k), by, start, size), :],
            r_buf[rows_at(shift(x, k) * depth, depth), columns],
            preferred_element_type=jnp.float32,
        )

    def unit(k, by, mode, start=0, size=None):
        size = quarter if size is None else size
        out_rows = rows_at(shift(x, by) * quarter + start, size, 32)

        def step(j, carry):
            columns = pl.ds(pl.multiple_of(j * TILE_N, TILE_N), TILE_N)
            value = product(k, by, start, size, columns)
            if mode != "set":
                value = value + c_buf[out_rows, columns]
            c_buf[out_rows, columns] = value
            if mode == "last":
                sq_sum[:, columns] += jnp.sum(value * value, axis=0, keepdims=True)
            return carry

        lax.fori_loop(0, cols // TILE_N, step, 0)

    def ext_value(h, mt, k):
        half_rows = quarter // 2
        if h == 0:
            block = shift(z, k)
            return jnp.dot(
                a_buf[a_part(block, -1, mt * half_rows, half_rows), :],
                r2_buf[rows_at(block * depth, depth), :],
                preferred_element_type=jnp.float32,
            )
        yy = shift(y, k)
        total = None
        for zz in range(SIDE):
            value = jnp.dot(
                a_buf[a_part(zz, 1, mt * half_rows, half_rows), pl.ds(pl.multiple_of(yy * chip, 128), chip)],
                r2_buf[rows_at(k_all + (zz * SIDE + yy) * chip, chip), :],
                preferred_element_type=jnp.float32,
            )
            total = value if total is None else total + value
        return total

    def ext_unit(h, k, mode):
        half_rows = quarter // 2

        def step(mt, carry):
            part = rows_at(mt * half_rows, half_rows)
            value = ext_value(h, mt, k)
            if mode != "set":
                value = value + ext[h, part, :]
            ext[h, part, :] = value
            if mode == "last":
                columns = pl.ds(h * side_cols, side_cols)
                sq_out[:, columns] += jnp.sum(value * value, axis=0, keepdims=True)
            return carry

        lax.fori_loop(0, 2, step, 0)

    def ext_copy(h):
        by = 1 - 2 * h
        dst = c_buf.at[rows_at(shift(x, -by) * quarter, quarter, 64), pl.ds(h * side_cols, side_cols)]
        return remote(ext.at[h], dst, sem["e_send"], sem["e_recv"], g, shift(x, by))

    def sq_ext_copy(h):
        columns = pl.ds(h * side_cols, side_cols)
        return remote(
            sq_out.at[:, columns], sq_in.at[:, columns], sem["q_send"], sem["q_recv"], g, shift(x, 1 - 2 * h)
        )

    own_rot.wait()
    for h in (0, 1):
        remote(
            r_buf.at[piece_rows(own, core), pl.ds(h * side_cols, side_cols)], r_ref(1, h, own, None, core),
            sem["x_send"], sem["x_recv"], g, shift(x, 2 * h - 1),
        ).start()
    r_own_first(0)
    own_coef.wait()
    for i in range(3):
        for direction in (0, 1):
            a_start(direction, i)
    r_own_second(0)
    sq_sum[...] = jnp.zeros_like(sq_sum)
    sq_out[...] = jnp.zeros_like(sq_out)
    for direction in (0, 1):
        for h in (0, 1):
            r_first(0, direction, h)
    for h in (0, 1):
        r_opposite(0, h)
    two = r2_buf.at[pl.ds(0, 2 * piece), :]
    remote(two, two, sem["x_send"], sem["x_recv"], g, shift(x, 1)).wait()
    r_own_first(1)
    r_own_second(1)
    for first in FIRSTS:
        for direction in (0, 1):
            for h in (0, 1):
                r_second(0, first, direction, h)
    for direction in (0, 1):
        a_wait(direction, 0)
        relay_start(direction)
    for first in FIRSTS:
        for h in (0, 1):
            r_second_opposite(0, first, h)
    pieces = SIDE * SIDE * piece
    ref = r_buf.at[pl.ds(0, pieces), :]
    remote(ref, ref, sem["p_send"], sem["p_recv"], partner, x).wait()
    for direction in (0, 1):
        for h in (0, 1):
            r_first(1, direction, h)
    for direction in (0, 1):
        a_wait(direction, 1)
        for c in range(len(LAST)):
            last_start(direction, c)

    unit(0, 0, "set")
    r_opposite(1, 0)
    unit(0, 1, "set")
    r_opposite(1, 1)
    unit(0, -1, "set")
    events = [(first, direction, h) for first in FIRSTS for direction in (0, 1) for h in (0, 1)]
    units = [(-1, 0), (1, 0), (-1, 1), (1, -1), None, (-1, -1), (1, 1)]
    for i, event in enumerate(events):
        r_second(1, *event)
        if i % 2 == 1 and i // 2 < len(units):
            if units[i // 2] is None:
                for direction in (0, 1):
                    a_wait(direction, 2)
            else:
                unit(*units[i // 2], "add")
    for direction in (0, 1):
        relay_wait(direction)
        unit(2, -1 if direction == 0 else 1, "last")
    early = r2_buf.at[pl.ds(0, 12 * piece), :]
    for h in (0, 1):
        remote(early, early, sem["t_send"], sem["p_recv%d0" % h], partner, x).wait_recv()
        for k in (0, -1, 1):
            ext_unit(h, k, "set" if k == 0 else "add")
        for first in FIRSTS[2 * h:2 * h + 2]:
            for hh in (0, 1):
                r_second_opposite(1, first, hh)
    late = r2_buf.at[pl.ds(0, 4 * piece), :]
    for h in (0, 1):
        remote(late, late, sem["t_send"], sem["p_recv%d1" % h], partner, x).wait_recv()
        ext_unit(h, 2, "last")
    for h in (0, 1):
        sq_ext_copy(h).start()
    for h in (0, 1):
        ext_copy(h).start()
    for c in range(len(LAST)):
        last_wait(c)
        unit(2, 0, "last", last_starts[c], LAST[c])
    remote(sq_out, sq_in, sem["q_send"], sem["q_recv"], g, shift(x, 1)).wait()

    sq_buf[g] = sq_sum[...] + sq_in[...]
    others = [(dz, dy, dc) for dz in range(-1, 3) for dy in range(-1, 3) for dc in (0, 1) if (dz, dy, dc) != (0, 0, 0)]
    for dz, dy, dc in sorted(others, key=lambda by: -(abs(by[0]) + abs(by[1]))):
        peer = device_of(shift(z, dz), shift(y, dy), (core + dc) % 2)
        remote(sq_buf.at[g], sq_buf.at[g], sem["s_send"] if False else load_sem.at[2], sem["t_recv"], peer, x).start()
    ref = a_buf.at[pl.ds(0, 9 * quarter), :]
    remote(ref, ref, sem["a_send"], sem["e_recv"], g, shift(x, 1)).wait_send()
    ref = r_buf.at[pl.ds(0, 15 * piece), :]
    remote(ref, ref, sem["r_send"], sem["e_recv"], partner, x).wait_send()
    ref = r2_buf.at[pl.ds(0, 30 * piece), :]
    remote(ref, ref, sem["s_send"], sem["e_recv"], partner, x).wait_send()
    ref = r2_buf.at[pl.ds(0, 32 * piece), :]
    remote(ref, ref, sem["t_send"], sem["e_recv"], partner, x).wait_send()
    ref = sq_buf.at[pl.ds(0, peers - 1)]
    remote(ref, ref, load_sem.at[2], sem["t_recv"], partner, x).wait()
    remote(ext, ext, sem["e_send"], sem["e_recv"], g, shift(x, 1)).wait()


def normalize(c_buf, sq_buf, out, rms_out, scale, staged, out_sem):
    rows, cols = c_buf.shape
    chunk = rows // CHUNKS
    total = sq_buf[0]
    for i in range(1, sq_buf.shape[0]):
        total = total + sq_buf[i]
    rms = jnp.sqrt(total / TOTAL_ROWS + 1e-06)
    rms_out[...] = rms.reshape(cols)
    scale[...] = 1.0 / rms

    def out_copy(c):
        part = pl.ds(c * chunk, chunk)
        return pltpu.make_async_copy(staged.at[part, :], out.at[part, :], out_sem.at[c])

    for c in range(CHUNKS):
        part = pl.ds(c * chunk, chunk)
        staged[part, :] = (c_buf[part, :] * scale[...]).astype(jnp.bfloat16)
        out_copy(c).start()
    for c in range(CHUNKS):
        out_copy(c).wait()


def body(coefficients, rotation):
    rows, depth = coefficients.shape
    piece, cols = rotation.shape
    peers = lax.axis_size("ga")
    dma = pltpu.SemaphoreType.DMA
    rotated, squares = pl.pallas_call(
        gather_multiply,
        out_shape=(pltpu.VMEM((rows, cols), jnp.float32), pltpu.VMEM((peers, 1, cols), jnp.float32)),
        in_specs=[pl.BlockSpec(memory_space=pl.ANY)] * 2,
        out_specs=(pl.BlockSpec(memory_space=pltpu.VMEM), pl.BlockSpec(memory_space=pltpu.VMEM)),
        scratch_shapes=[
            pltpu.VMEM((SIDE * rows, depth), jnp.bfloat16),
            pltpu.VMEM((SIDE * depth, cols), jnp.bfloat16),
            pltpu.VMEM((2 * SIDE * depth, cols // 2), jnp.bfloat16),
            pltpu.VMEM((2, rows // SIDE, cols // 2), jnp.float32),
            pltpu.VMEM((1, cols), jnp.float32),
            pltpu.VMEM((1, cols), jnp.float32),
            pltpu.VMEM((1, cols), jnp.float32),
            dma((3,)),
            dma((2, 3)),
            dma((2,)),
            dma((len(LAST),)),
            dma((2, 15)),
            dma((2, 15)),
            dma((len(SEMS),)),
        ],
        compiler_params=pltpu.CompilerParams(
            collective_id=0, has_side_effects=True, vmem_limit_bytes=55 * 1024 * 1024
        ),
        cost_estimate=pl.CostEstimate(
            flops=2 * rows * depth * SIDE * cols, bytes_accessed=4 * rows * depth, transcendentals=0
        ),
    )(coefficients, rotation)
    return pl.pallas_call(
        normalize,
        out_shape=(
            jax.ShapeDtypeStruct((rows, cols), jnp.bfloat16),
            jax.ShapeDtypeStruct((cols,), jnp.float32),
        ),
        in_specs=[pl.BlockSpec(memory_space=pltpu.VMEM)] * 2,
        out_specs=(pl.BlockSpec(memory_space=pl.ANY), pl.BlockSpec(memory_space=pltpu.VMEM)),
        scratch_shapes=[
            pltpu.VMEM((1, cols), jnp.float32),
            pltpu.VMEM((rows, cols), jnp.bfloat16),
            dma((CHUNKS,)),
        ],
        compiler_params=pltpu.CompilerParams(vmem_limit_bytes=20 * 1024 * 1024),
        cost_estimate=pl.CostEstimate(flops=rows * cols, bytes_accessed=6 * rows * cols, transcendentals=0),
    )(rotated, squares)


def solution(mesh):
    return jax.shard_map(
        body, mesh=mesh, in_specs=(P("ga", "ba"), P("ga", "ba")), out_specs=(P("ga", "ba"), P("ba")), check_vma=False
    )
```

time: 148 us -> 148 us (level)
  no operation moved by 1% of the time
where the time goes in v4:
time: 148 us
  Pallas kernels  147 us (99%)
    pallas_call x1, Pallas kernels, body(): pl.pallas_call(gather_multiply, out_shape=(pltpu.VMEM((rows, cols), jnp.f...  144 us

profile of v4, /device:TPU:1, one launch (start us, length us, event | category | flops | bytes accessed | tf_op | source)
XLA Modules:
  0.0 147.8 jit_solution(8434114101026331081)
XLA Ops:
  0.6 144.4 %shard_map.41 = (f32[1280,1536]{1,0:T(8,128)S(1)}, f32[32,1,1536]{2,1,0:T(1,128)S(1)}) custom-call(bf16[1280,1536]{1,0:T(8,128)(2,1)} %coef.1, bf16[192,1536]{1,0:T(8,128)(2,1)} %rot.1), custom_call_target="tpu_custom_call" | custom-call | flops 24159191040 | bytes 7864320 | tf_op jit(solution)/shard_map/pallas_call | solution.py:392
  145.0 2.7 %shard_map.42 = (bf16[1280,1536]{1,0:T(8,128)(2,1)}, f32[1536]{0:T(1024)}) custom-call(f32[1280,1536]{1,0:T(8,128)S(1)} %get-tuple-element.4.c_buf, f32[32,1,1536]{2,1,0:T(1,128)S(1)} %get-tuple-element.5.sq_buf), custom_call_target="tpu_custom_call" | custom-call | flops 1966080 | bytes 11796480 | tf_op jit(solution)/shard_map/pallas_call | solution.py:420

commit v5 on v4

--- a/solution.py
+++ b/solution.py
@@ -9,10 +9,10 @@
 SIDE = 4
 LAST = (256, 64)
 CHUNKS = 8
-TILE_N = 512
+TILE_N = 768
 TOTAL_ROWS = 40960
-SENDS = ("a_send", "r_send", "s_send", "p_send", "x_send", "e_send", "q_send", "t_send")
-ARRIVALS = ("x_recv", "e_recv", "q_recv", "t_recv", "p_recv", "p_recv00", "p_recv01", "p_recv10", "p_recv11")
+SENDS = ("a_send", "r_send", "r2_send", "p_send", "p2_send", "x_send", "e_send", "q_send", "s_send")
+ARRIVALS = ("x_recv", "e_recv", "q_recv", "s_recv", "p_recv", "p_recv00", "p_recv01", "p_recv10", "p_recv11")
 SEMS = {name: i for i, name in enumerate(SENDS + ARRIVALS)}
 
 
@@ -129,7 +129,7 @@
     def r_start(q, h, at, part, slot, to):
         ref = r_ref(q, h, at, part, core)
         recv = (r_sem if q == 0 else r2_sem).at[h, slot]
-        remote(ref, ref, sem["r_send"] if q == 0 else sem["s_send"], recv, device_of(to[0], to[1], core), x).start()
+        remote(ref, ref, sem["r_send"] if q == 0 else sem["r2_send"], recv, device_of(to[0], to[1], core), x).start()
 
     def r_wait(q, h, at, slot):
         ref = r_ref(q, h, at, None, core)
@@ -139,15 +139,12 @@
     def to_partner(q, h, at, late):
         ref = r_ref(q, h, at, None, core)
         recv = sem["p_recv"] if q == 0 else sem["p_recv%d%d" % (h, late)]
-        remote(ref, ref, sem["p_send"] if q == 0 else sem["t_send"], recv, partner, x).start()
+        remote(ref, ref, sem["p_send"] if q == 0 else sem["p2_send"], recv, partner, x).start()
 
     places = {0: 0, -1: 1, 1: 2, 2: 3}
 
     def slot_of(first, kind):
         return 3 + 3 * places[first] + kind
-
-    def late_of(first):
-        return 0
 
     def along_second(q, h, at, first):
         for direction in (0, 1):
@@ -163,13 +160,18 @@
             along_second(q, h, own, 0)
             to_partner(q, h, own, 0)
 
-    def r_first(q, direction, h):
-        by = 1 - 2 * direction
-        at = place(h, -by, 0)
-        r_wait(q, h, at, direction)
-        r_start(q, h, at, direction, 2, place(h, by, 0))
-        along_second(q, h, at, -by)
-        to_partner(q, h, at, 0)
+    def r_first(q):
+        for direction in (0, 1):
+            by = 1 - 2 * direction
+            for h in (0, 1):
+                at = place(h, -by, 0)
+                r_wait(q, h, at, direction)
+                r_start(q, h, at, direction, 2, place(h, by, 0))
+        for by in (1, -1):
+            for h in (0, 1):
+                at = place(h, -by, 0)
+                along_second(q, h, at, -by)
+                to_partner(q, h, at, 0)
 
     def r_opposite(q, h):
         at = place(h, 2, 0)
@@ -275,70 +277,69 @@
     r_own_second(0)
     sq_sum[...] = jnp.zeros_like(sq_sum)
     sq_out[...] = jnp.zeros_like(sq_out)
-    for direction in (0, 1):
-        for h in (0, 1):
-            r_first(0, direction, h)
+    r_first(0)
     for h in (0, 1):
         r_opposite(0, h)
+    for first in FIRSTS:
+        for direction in (0, 1):
+            for h in (0, 1):
+                r_second(0, first, direction, h)
     two = r2_buf.at[pl.ds(0, 2 * piece), :]
     remote(two, two, sem["x_send"], sem["x_recv"], g, shift(x, 1)).wait()
     r_own_first(1)
     r_own_second(1)
-    for first in FIRSTS:
-        for direction in (0, 1):
-            for h in (0, 1):
-                r_second(0, first, direction, h)
     for direction in (0, 1):
         a_wait(direction, 0)
         relay_start(direction)
     for first in FIRSTS:
         for h in (0, 1):
             r_second_opposite(0, first, h)
-    pieces = SIDE * SIDE * piece
-    ref = r_buf.at[pl.ds(0, pieces), :]
-    remote(ref, ref, sem["p_send"], sem["p_recv"], partner, x).wait()
-    for direction in (0, 1):
-        for h in (0, 1):
-            r_first(1, direction, h)
     for direction in (0, 1):
         a_wait(direction, 1)
         for c in range(len(LAST)):
             last_start(direction, c)
+    pieces = SIDE * SIDE * piece
+    ref = r_buf.at[pl.ds(0, pieces), :]
+    remote(ref, ref, sem["p_send"], sem["p_recv"], partner, x).wait()
 
     unit(0, 0, "set")
+    unit(0, 1, "set")
+    r_first(1)
+    unit(0, -1, "set")
+    for k in (-1, 1):
+        unit(k, 0, "add")
     r_opposite(1, 0)
-    unit(0, 1, "set")
+    for k in (-1, 1):
+        unit(k, -k, "add")
     r_opposite(1, 1)
-    unit(0, -1, "set")
-    events = [(first, direction, h) for first in FIRSTS for direction in (0, 1) for h in (0, 1)]
-    units = [(-1, 0), (1, 0), (-1, 1), (1, -1), None, (-1, -1), (1, 1)]
-    for i, event in enumerate(events):
-        r_second(1, *event)
-        if i % 2 == 1 and i // 2 < len(units):
-            if units[i // 2] is None:
-                for direction in (0, 1):
-                    a_wait(direction, 2)
-            else:
-                unit(*units[i // 2], "add")
+    for first in FIRSTS:
+        for direction in (0, 1):
+            for h in (0, 1):
+                r_second(1, first, direction, h)
+        if first == 0:
+            for direction, k in enumerate((-1, 1)):
+                a_wait(direction, 2)
+                unit(k, k, "add")
     for direction in (0, 1):
         relay_wait(direction)
-        unit(2, -1 if direction == 0 else 1, "last")
     early = r2_buf.at[pl.ds(0, 12 * piece), :]
     for h in (0, 1):
-        remote(early, early, sem["t_send"], sem["p_recv%d0" % h], partner, x).wait_recv()
+        remote(early, early, sem["p2_send"], sem["p_recv%d0" % h], partner, x).wait_recv()
         for k in (0, -1, 1):
             ext_unit(h, k, "set" if k == 0 else "add")
-        for first in FIRSTS[2 * h:2 * h + 2]:
-            for hh in (0, 1):
-                r_second_opposite(1, first, hh)
+    for h in (0, 1):
+        for first in FIRSTS:
+            r_second_opposite(1, first, h)
     late = r2_buf.at[pl.ds(0, 4 * piece), :]
     for h in (0, 1):
-        remote(late, late, sem["t_send"], sem["p_recv%d1" % h], partner, x).wait_recv()
+        remote(late, late, sem["p2_send"], sem["p_recv%d1" % h], partner, x).wait_recv()
         ext_unit(h, 2, "last")
     for h in (0, 1):
         sq_ext_copy(h).start()
     for h in (0, 1):
         ext_copy(h).start()
+    for by in (-1, 1):
+        unit(2, by, "last")
     for c in range(len(LAST)):
         last_wait(c)
         unit(2, 0, "last", last_starts[c], LAST[c])
@@ -348,17 +349,17 @@
     others = [(dz, dy, dc) for dz in range(-1, 3) for dy in range(-1, 3) for dc in (0, 1) if (dz, dy, dc) != (0, 0, 0)]
     for dz, dy, dc in sorted(others, key=lambda by: -(abs(by[0]) + abs(by[1]))):
         peer = device_of(shift(z, dz), shift(y, dy), (core + dc) % 2)
-        remote(sq_buf.at[g], sq_buf.at[g], sem["s_send"] if False else load_sem.at[2], sem["t_recv"], peer, x).start()
+        remote(sq_buf.at[g], sq_buf.at[g], sem["s_send"], sem["s_recv"], peer, x).start()
     ref = a_buf.at[pl.ds(0, 9 * quarter), :]
     remote(ref, ref, sem["a_send"], sem["e_recv"], g, shift(x, 1)).wait_send()
     ref = r_buf.at[pl.ds(0, 15 * piece), :]
     remote(ref, ref, sem["r_send"], sem["e_recv"], partner, x).wait_send()
     ref = r2_buf.at[pl.ds(0, 30 * piece), :]
-    remote(ref, ref, sem["s_send"], sem["e_recv"], partner, x).wait_send()
+    remote(ref, ref, sem["r2_send"], sem["e_recv"], partner, x).wait_send()
     ref = r2_buf.at[pl.ds(0, 32 * piece), :]
-    remote(ref, ref, sem["t_send"], sem["e_recv"], partner, x).wait_send()
+    remote(ref, ref, sem["p2_send"], sem["e_recv"], partner, x).wait_send()
     ref = sq_buf.at[pl.ds(0, peers - 1)]
-    remote(ref, ref, load_sem.at[2], sem["t_recv"], partner, x).wait()
+    remote(ref, ref, sem["s_send"], sem["s_recv"], partner, x).wait()
     remote(ext, ext, sem["e_send"], sem["e_recv"], g, shift(x, 1)).wait()
 
 
@@ -402,7 +403,7 @@
             pltpu.VMEM((1, cols), jnp.float32),
             pltpu.VMEM((1, cols), jnp.float32),
             pltpu.VMEM((1, cols), jnp.float32),
-            dma((3,)),
+            dma((2,)),
             dma((2, 3)),
             dma((2,)),
             dma((len(LAST),)),

time: 148 us -> 138 us (0.932)
  Pallas kernels: 147 us -> 138 us
    pallas_call x1, Pallas kernels: 144 us -> 135 us  [body(): pl.pallas_call(gather_multiply, out_shape=(pltpu.VMEM((rows, cols), jnp.f...]
where the time goes in v5:
time: 138 us
  Pallas kernels  138 us (100%)
    pallas_call x1, Pallas kernels, body(): pl.pallas_call(gather_multiply, out_shape=(pltpu.VMEM((rows, cols), jnp.f...  135 us

profile of v5, /device:TPU:1, one launch (start us, length us, event | category | flops | bytes accessed | tf_op | source)
XLA Modules:
  0.0 138.2 jit_solution(12918722648662797406)
XLA Ops:
  0.6 134.8 %shard_map.41 = (f32[1280,1536]{1,0:T(8,128)S(1)}, f32[32,1,1536]{2,1,0:T(1,128)S(1)}) custom-call(bf16[1280,1536]{1,0:T(8,128)(2,1)} %coef.1, bf16[192,1536]{1,0:T(8,128)(2,1)} %rot.1), custom_call_target="tpu_custom_call" | custom-call | flops 24159191040 | bytes 7864320 | tf_op jit(solution)/shard_map/pallas_call | solution.py:393
  135.5 2.7 %shard_map.42 = (bf16[1280,1536]{1,0:T(8,128)(2,1)}, f32[1536]{0:T(1024)}) custom-call(f32[1280,1536]{1,0:T(8,128)S(1)} %get-tuple-element.4.c_buf, f32[32,1,1536]{2,1,0:T(1,128)S(1)} %get-tuple-element.5.sq_buf), custom_call_target="tpu_custom_call" | custom-call | flops 1966080 | bytes 11796480 | tf_op jit(solution)/shard_map/pallas_call | solution.py:421

commit v6 on v5

--- a/solution.py
+++ b/solution.py
@@ -7,17 +7,18 @@
 
 MESH = pl.DeviceIdType.MESH
 SIDE = 4
-LAST = (256, 64)
-CHUNKS = 8
+LAST = (320,)
+WIDE = 128
 TILE_N = 768
+EXT_M = 160
 TOTAL_ROWS = 40960
-SENDS = ("a_send", "r_send", "r2_send", "p_send", "p2_send", "x_send", "e_send", "q_send", "s_send")
-ARRIVALS = ("x_recv", "e_recv", "q_recv", "s_recv", "p_recv", "p_recv00", "p_recv01", "p_recv10", "p_recv11")
+SENDS = ("a_send", "r_send", "r2_send", "p_send", "p2_send", "x_send", "e_send", "q_send", "s_send", "n_send", "b_send")
+ARRIVALS = ("x_recv", "e_recv", "q_recv", "s_recv", "n_recv", "b_recv", "p_recv", "p_recv00", "p_recv01", "p_recv10", "p_recv11")
 SEMS = {name: i for i, name in enumerate(SENDS + ARRIVALS)}
 
 
 def gather_multiply(
-    coef, rot, c_buf, sq_buf, a_buf, r_buf, r2_buf, ext, sq_sum, sq_out, sq_in,
+    coef, rot, c_buf, rms_out, scale, narrow, a_buf, r_buf, r2_buf, ext, sq_buf, sq_sum, sq_out, sq_in, scale_in,
     load_sem, a_sem, relay_sem, last_sem, r_sem, r2_sem, sems,
 ):
     rows, depth = coef.shape
@@ -216,32 +217,34 @@
 
         lax.fori_loop(0, cols // TILE_N, step, 0)
 
-    def ext_value(h, mt, k):
-        half_rows = quarter // 2
-        if h == 0:
-            block = shift(z, k)
-            return jnp.dot(
-                a_buf[a_part(block, -1, mt * half_rows, half_rows), :],
-                r2_buf[rows_at(block * depth, depth), :],
-                preferred_element_type=jnp.float32,
-            )
-        yy = shift(y, k)
+    delta = (x + 2 - z + SIDE) % SIDE
+    low = 1 - delta // 2
+    early_blocks = ((3 - delta) // 3, 1 + 2 * low)
+    late_blocks = (delta * low + 3 * (1 - low), 2)
+
+    def ext_dot_0(start, block):
+        return jnp.dot(
+            a_buf[a_part(block, -1, start, EXT_M), :],
+            r2_buf[rows_at(block * depth, depth), :],
+            preferred_element_type=jnp.float32,
+        )
+
+    def ext_dot_1(start, pairs):
         total = None
-        for zz in range(SIDE):
+        for zz, yy in pairs:
             value = jnp.dot(
-                a_buf[a_part(zz, 1, mt * half_rows, half_rows), pl.ds(pl.multiple_of(yy * chip, 128), chip)],
+                a_buf[a_part(zz, 1, start, EXT_M), pl.ds(pl.multiple_of(yy * chip, 128), chip)],
                 r2_buf[rows_at(k_all + (zz * SIDE + yy) * chip, chip), :],
                 preferred_element_type=jnp.float32,
             )
             total = value if total is None else total + value
         return total
 
-    def ext_unit(h, k, mode):
-        half_rows = quarter // 2
-
-        def step(mt, carry):
-            part = rows_at(mt * half_rows, half_rows)
-            value = ext_value(h, mt, k)
+    def ext_unit(h, dot, what, mode):
+        def step(i, carry):
+            start = pl.multiple_of(i * EXT_M, EXT_M)
+            part = pl.ds(start, EXT_M)
+            value = dot(start, what)
             if mode != "set":
                 value = value + ext[h, part, :]
             ext[h, part, :] = value
@@ -250,12 +253,42 @@
                 sq_out[:, columns] += jnp.sum(value * value, axis=0, keepdims=True)
             return carry
 
-        lax.fori_loop(0, 2, step, 0)
+        lax.fori_loop(0, quarter // EXT_M, step, 0)
+
+    def ext_early(h):
+        if h == 0:
+            for i, k in enumerate(early_blocks):
+                ext_unit(0, ext_dot_0, shift(z, k), "set" if i == 0 else "add")
+        else:
+            for i, k in enumerate((0, -1, 1)):
+                pairs = [(shift(x, b), shift(y, k)) for b in (0, -1, 1)]
+                ext_unit(1, ext_dot_1, pairs, "set" if i == 0 else "add")
+
+    def ext_late(h):
+        if h == 0:
+            for i, k in enumerate(late_blocks):
+                ext_unit(0, ext_dot_0, shift(z, k), "add" if i == 0 else "last")
+        else:
+            pairs = [(shift(x, 2), shift(y, k)) for k in (0, -1, 1)] + [(zz, shift(y, 2)) for zz in range(SIDE)]
+            ext_unit(1, ext_dot_1, pairs, "last")
 
     def ext_copy(h):
         by = 1 - 2 * h
-        dst = c_buf.at[rows_at(shift(x, -by) * quarter, quarter, 64), pl.ds(h * side_cols, side_cols)]
-        return remote(ext.at[h], dst, sem["e_send"], sem["e_recv"], g, shift(x, by))
+        dst = c_buf.at[rows_at(shift(x, -by) * quarter, WIDE, 64), pl.ds(h * side_cols, side_cols)]
+        return remote(ext.at[h, pl.ds(0, WIDE), :], dst, sem["e_send"], sem["e_recv"], g, shift(x, by))
+
+    def rounded(h, count=1):
+        return r2_buf.at[pl.ds(h * (quarter - WIDE), count * (quarter - WIDE)), :]
+
+    def rounded_copy(h):
+        dst = narrow.at[:, pl.ds(h * side_cols, side_cols)]
+        return remote(rounded(h), dst, sem["b_send"], sem["b_recv"], g, shift(x, 1 - 2 * h))
+
+    def scale_copy(h):
+        columns = pl.ds(h * side_cols, side_cols)
+        return remote(
+            scale.at[:, columns], scale_in.at[:, columns], sem["n_send"], sem["n_recv"], g, shift(x, 2 * h - 1)
+        )
 
     def sq_ext_copy(h):
         columns = pl.ds(h * side_cols, side_cols)
@@ -320,26 +353,23 @@
             for direction, k in enumerate((-1, 1)):
                 a_wait(direction, 2)
                 unit(k, k, "add")
-    for direction in (0, 1):
+    early = r2_buf.at[pl.ds(0, 12 * piece), :]
+    for h in (0, 1):
+        remote(early, early, sem["p2_send"], sem["p_recv%d0" % h], partner, x).wait_recv()
+        ext_early(h)
+    for direction, by in enumerate((-1, 1)):
         relay_wait(direction)
-    early = r2_buf.at[pl.ds(0, 12 * piece), :]
-    for h in (0, 1):
-        remote(early, early, sem["p2_send"], sem["p_recv%d0" % h], partner, x).wait_recv()
-        for k in (0, -1, 1):
-            ext_unit(h, k, "set" if k == 0 else "add")
-    for h in (0, 1):
-        for first in FIRSTS:
-            r_second_opposite(1, first, h)
+        unit(2, by, "last")
+        for first in FIRSTS[2 * direction:2 * direction + 2]:
+            for h in (0, 1):
+                r_second_opposite(1, first, h)
     late = r2_buf.at[pl.ds(0, 4 * piece), :]
     for h in (0, 1):
         remote(late, late, sem["p2_send"], sem["p_recv%d1" % h], partner, x).wait_recv()
-        ext_unit(h, 2, "last")
-    for h in (0, 1):
+        ext_late(h)
         sq_ext_copy(h).start()
     for h in (0, 1):
         ext_copy(h).start()
-    for by in (-1, 1):
-        unit(2, by, "last")
     for c in range(len(LAST)):
         last_wait(c)
         unit(2, 0, "last", last_starts[c], LAST[c])
@@ -360,29 +390,48 @@
     remote(ref, ref, sem["p2_send"], sem["e_recv"], partner, x).wait_send()
     ref = sq_buf.at[pl.ds(0, peers - 1)]
     remote(ref, ref, sem["s_send"], sem["s_recv"], partner, x).wait()
-    remote(ext, ext, sem["e_send"], sem["e_recv"], g, shift(x, 1)).wait()
-
-
-def normalize(c_buf, sq_buf, out, rms_out, scale, staged, out_sem):
-    rows, cols = c_buf.shape
-    chunk = rows // CHUNKS
     total = sq_buf[0]
-    for i in range(1, sq_buf.shape[0]):
+    for i in range(1, peers):
         total = total + sq_buf[i]
     rms = jnp.sqrt(total / TOTAL_ROWS + 1e-06)
-    rms_out[...] = rms.reshape(cols)
+    rms_out[...] = rms
     scale[...] = 1.0 / rms
-
-    def out_copy(c):
-        part = pl.ds(c * chunk, chunk)
-        return pltpu.make_async_copy(staged.at[part, :], out.at[part, :], out_sem.at[c])
-
-    for c in range(CHUNKS):
-        part = pl.ds(c * chunk, chunk)
-        staged[part, :] = (c_buf[part, :] * scale[...]).astype(jnp.bfloat16)
-        out_copy(c).start()
-    for c in range(CHUNKS):
-        out_copy(c).wait()
+    for h in (0, 1):
+        scale_copy(h).start()
+    remote(scale, scale_in, sem["n_send"], sem["n_recv"], g, shift(x, 1)).wait()
+    for h in (0, 1):
+        rounded(h)[...] = (ext[h, WIDE:, :] * scale_in[:, h * side_cols:(h + 1) * side_cols]).astype(jnp.bfloat16)
+        rounded_copy(h).start()
+    ref = ext.at[:, pl.ds(0, WIDE), :]
+    remote(ref, ref, sem["e_send"], sem["e_recv"], g, shift(x, 1)).wait()
+    remote(rounded(0, 2), rounded(0, 2), sem["b_send"], sem["b_recv"], g, shift(x, 1)).wait()
+
+
+def normalize(c_buf, rms_in, scale, narrow, out, rms_out, staged, out_sem):
+    rows, cols = c_buf.shape
+    quarter = rows // SIDE
+    x = lax.axis_index("ba")
+    rms_out[...] = rms_in[...].reshape(cols)
+    copies = []
+
+    def put(src, start, size):
+        part = pl.ds(pl.multiple_of(start, 64), size)
+        copy = pltpu.make_async_copy(src, out.at[part, :], out_sem.at[len(copies)])
+        copy.start()
+        copies.append(copy)
+
+    def opposite(by):
+        return (x + by) % SIDE * quarter
+
+    put(narrow, opposite(2) + WIDE, quarter - WIDE)
+    at = 0
+    for by, start, size in [(2, 0, WIDE)] + [(by, start, 64) for by in (0, 1, 3) for start in range(0, quarter, 64)]:
+        part = pl.ds(pl.multiple_of(opposite(by) + start, 64), size)
+        staged[pl.ds(at, size), :] = (c_buf[part, :] * scale[...]).astype(jnp.bfloat16)
+        put(staged.at[pl.ds(at, size), :], opposite(by) + start, size)
+        at += size
+    for copy in copies:
+        copy.wait()
 
 
 def body(coefficients, rotation):
@@ -390,19 +439,25 @@
     piece, cols = rotation.shape
     peers = lax.axis_size("ga")
     dma = pltpu.SemaphoreType.DMA
-    rotated, squares = pl.pallas_call(
+    row = pltpu.VMEM((1, cols), jnp.float32)
+    parts = pl.pallas_call(
         gather_multiply,
-        out_shape=(pltpu.VMEM((rows, cols), jnp.float32), pltpu.VMEM((peers, 1, cols), jnp.float32)),
+        out_shape=(
+            pltpu.VMEM((rows, cols), jnp.float32), row, row,
+            pltpu.VMEM((rows // SIDE - WIDE, cols), jnp.bfloat16),
+        ),
         in_specs=[pl.BlockSpec(memory_space=pl.ANY)] * 2,
-        out_specs=(pl.BlockSpec(memory_space=pltpu.VMEM), pl.BlockSpec(memory_space=pltpu.VMEM)),
+        out_specs=(pl.BlockSpec(memory_space=pltpu.VMEM),) * 4,
         scratch_shapes=[
             pltpu.VMEM((SIDE * rows, depth), jnp.bfloat16),
             pltpu.VMEM((SIDE * depth, cols), jnp.bfloat16),
             pltpu.VMEM((2 * SIDE * depth, cols // 2), jnp.bfloat16),
             pltpu.VMEM((2, rows // SIDE, cols // 2), jnp.float32),
-            pltpu.VMEM((1, cols), jnp.float32),
-            pltpu.VMEM((1, cols), jnp.float32),
-            pltpu.VMEM((1, cols), jnp.float32),
+            pltpu.VMEM((peers, 1, cols), jnp.float32),
+            row,
+            row,
+            row,
+            row,
             dma((2,)),
             dma((2, 3)),
             dma((2,)),
@@ -424,16 +479,15 @@
             jax.ShapeDtypeStruct((rows, cols), jnp.bfloat16),
             jax.ShapeDtypeStruct((cols,), jnp.float32),
         ),
-        in_specs=[pl.BlockSpec(memory_space=pltpu.VMEM)] * 2,
+        in_specs=[pl.BlockSpec(memory_space=pltpu.VMEM)] * 4,
         out_specs=(pl.BlockSpec(memory_space=pl.ANY), pl.BlockSpec(memory_space=pltpu.VMEM)),
         scratch_shapes=[
-            pltpu.VMEM((1, cols), jnp.float32),
             pltpu.VMEM((rows, cols), jnp.bfloat16),
-            dma((CHUNKS,)),
+            dma((20,)),
         ],
         compiler_params=pltpu.CompilerParams(vmem_limit_bytes=20 * 1024 * 1024),
         cost_estimate=pl.CostEstimate(flops=rows * cols, bytes_accessed=6 * rows * cols, transcendentals=0),
-    )(rotated, squares)
+    )(*parts)
 
 
 def solution(mesh):

time: 138 us -> 134 us (0.971)
  Pallas kernels: 138 us -> 133 us
    pallas_call x1, Pallas kernels: 135 us -> 131 us  [body(): pl.pallas_call(gather_multiply, out_shape=(pltpu.VMEM((rows, cols), jnp.f...]
where the time goes in v6:
time: 134 us
  Pallas kernels  133 us (99%)
    pallas_call x1, Pallas kernels, body(): pl.pallas_call(gather_multiply, out_shape=(pltpu.VMEM((rows, cols), jnp.f...  131 us
    pallas_call x1, Pallas kernels, body(): pl.pallas_call(normalize, out_shape=(jax.ShapeDtypeStruct((rows, cols), j...  2.68 us

profile of v6, /device:TPU:1, one launch (start us, length us, event | category | flops | bytes accessed | tf_op | source)
XLA Modules:
  0.0 134.0 jit_solution(14992764450539487124)
XLA Ops:
  0.6 130.7 %shard_map.41 = (f32[1280,1536]{1,0:T(8,128)S(1)}, f32[1,1536]{1,0:T(1,128)S(1)}, f32[1,1536]{1,0:T(1,128)S(1)}, bf16[192,1536]{1,0:T(8,128)(2,1)S(1)}) custom-call(bf16[1280,1536]{1,0:T(8,128)(2,1)} %coef.1, bf16[192,1536]{1,0:T(8,128)(2,1)} %rot.1), custom_call_target="tpu_custom_call" | custom-call | flops 24159191040 | bytes 7864320 | tf_op jit(solution)/shard_map/pallas_call | solution.py:443
  131.3 2.7 %shard_map.42 = (bf16[1280,1536]{1,0:T(8,128)(2,1)}, f32[1536]{0:T(1024)}) custom-call(f32[1280,1536]{1,0:T(8,128)S(1)} %get-tuple-element.6.c_buf, f32[1,1536]{1,0:T(1,128)S(1)} %get-tuple-element.7.rms_in, f32[1,1536]{1,0:T(1,128)S(1)} %get-tuple-element.8.scale, bf16[192,1536]{1,0:T(8,128)(2,1)S(1)} %get-tuple-element.9.narrow), custom_call_target="tpu_custom_call" | custom-call | flops 1966080 | bytes 11796480 | tf_op jit(solution)/shard_map/pallas_call | solution.py:476

commit v7 on v6

--- a/solution.py
+++ b/solution.py
@@ -8,7 +8,7 @@
 MESH = pl.DeviceIdType.MESH
 SIDE = 4
 LAST = (320,)
-WIDE = 128
+FIRST_WIDE, WIDE = 128, 176
 TILE_N = 768
 EXT_M = 160
 TOTAL_ROWS = 40960
@@ -264,18 +264,21 @@
                 pairs = [(shift(x, b), shift(y, k)) for b in (0, -1, 1)]
                 ext_unit(1, ext_dot_1, pairs, "set" if i == 0 else "add")
 
+    def ext_middle():
+        ext_unit(0, ext_dot_0, shift(z, late_blocks[0]), "add")
+        ext_unit(1, ext_dot_1, [(shift(x, 2), shift(y, k)) for k in (0, -1, 1)], "add")
+
     def ext_late(h):
         if h == 0:
-            for i, k in enumerate(late_blocks):
-                ext_unit(0, ext_dot_0, shift(z, k), "add" if i == 0 else "last")
+            ext_unit(0, ext_dot_0, shift(z, late_blocks[1]), "last")
         else:
-            pairs = [(shift(x, 2), shift(y, k)) for k in (0, -1, 1)] + [(zz, shift(y, 2)) for zz in range(SIDE)]
-            ext_unit(1, ext_dot_1, pairs, "last")
-
-    def ext_copy(h):
+            ext_unit(1, ext_dot_1, [(zz, shift(y, 2)) for zz in range(SIDE)], "last")
+
+    def ext_copy(h, start, stop):
         by = 1 - 2 * h
-        dst = c_buf.at[rows_at(shift(x, -by) * quarter, WIDE, 64), pl.ds(h * side_cols, side_cols)]
-        return remote(ext.at[h, pl.ds(0, WIDE), :], dst, sem["e_send"], sem["e_recv"], g, shift(x, by))
+        dst = c_buf.at[rows_at(shift(x, -by) * quarter + start, stop - start, 64), pl.ds(h * side_cols, side_cols)]
+        src = ext.at[h, pl.ds(start, stop - start), :]
+        return remote(src, dst, sem["e_send"], sem["e_recv"], g, shift(x, by))
 
     def rounded(h, count=1):
         return r2_buf.at[pl.ds(h * (quarter - WIDE), count * (quarter - WIDE)), :]
@@ -363,13 +366,13 @@
         for first in FIRSTS[2 * direction:2 * direction + 2]:
             for h in (0, 1):
                 r_second_opposite(1, first, h)
+    ext_middle()
     late = r2_buf.at[pl.ds(0, 4 * piece), :]
     for h in (0, 1):
         remote(late, late, sem["p2_send"], sem["p_recv%d1" % h], partner, x).wait_recv()
         ext_late(h)
         sq_ext_copy(h).start()
-    for h in (0, 1):
-        ext_copy(h).start()
+        ext_copy(h, 0, FIRST_WIDE).start()
     for c in range(len(LAST)):
         last_wait(c)
         unit(2, 0, "last", last_starts[c], LAST[c])
@@ -398,6 +401,7 @@
     scale[...] = 1.0 / rms
     for h in (0, 1):
         scale_copy(h).start()
+        ext_copy(h, FIRST_WIDE, WIDE).start()
     remote(scale, scale_in, sem["n_send"], sem["n_recv"], g, shift(x, 1)).wait()
     for h in (0, 1):
         rounded(h)[...] = (ext[h, WIDE:, :] * scale_in[:, h * side_cols:(h + 1) * side_cols]).astype(jnp.bfloat16)
@@ -415,7 +419,7 @@
     copies = []
 
     def put(src, start, size):
-        part = pl.ds(pl.multiple_of(start, 64), size)
+        part = pl.ds(pl.multiple_of(start, 16), size)
         copy = pltpu.make_async_copy(src, out.at[part, :], out_sem.at[len(copies)])
         copy.start()
         copies.append(copy)

time: 134 us -> 133 us (level)
    pallas_call x1, Pallas kernels: 131 us -> 129 us  [body(): pl.pallas_call(gather_multiply, out_shape=(pltpu.VMEM((rows, cols), jnp.f...]
where the time goes in v7:
time: 133 us; the launch traced here: 132 us
  Pallas kernels  132 us (99%)
    pallas_call x1, Pallas kernels, body(): pl.pallas_call(gather_multiply, out_shape=(pltpu.VMEM((rows, cols), jnp.f...  129 us
    pallas_call x1, Pallas kernels, body(): pl.pallas_call(normalize, out_shape=(jax.ShapeDtypeStruct((rows, cols), j...  2.68 us

profile of v7, /device:TPU:1, one launch (start us, length us, event | category | flops | bytes accessed | tf_op | source)
XLA Modules:
  0.0 132.4 jit_solution(1374989632315499519)
XLA Ops:
  0.6 129.0 %shard_map.41 = (f32[1280,1536]{1,0:T(8,128)S(1)}, f32[1,1536]{1,0:T(1,128)S(1)}, f32[1,1536]{1,0:T(1,128)S(1)}, bf16[144,1536]{1,0:T(8,128)(2,1)S(1)}) custom-call(bf16[1280,1536]{1,0:T(8,128)(2,1)} %coef.1, bf16[192,1536]{1,0:T(8,128)(2,1)} %rot.1), custom_call_target="tpu_custom_call" | custom-call | flops 24159191040 | bytes 7864320 | tf_op jit(solution)/shard_map/pallas_call | solution.py:447
  129.7 2.7 %shard_map.42 = (bf16[1280,1536]{1,0:T(8,128)(2,1)}, f32[1536]{0:T(1024)}) custom-call(f32[1280,1536]{1,0:T(8,128)S(1)} %get-tuple-element.6.c_buf, f32[1,1536]{1,0:T(1,128)S(1)} %get-tuple-element.7.rms_in, f32[1,1536]{1,0:T(1,128)S(1)} %get-tuple-element.8.scale, bf16[144,1536]{1,0:T(8,128)(2,1)S(1)} %get-tuple-element.9.narrow), custom_call_target="tpu_custom_call" | custom-call | flops 1966080 | bytes 11796480 | tf_op jit(solution)/shard_map/pallas_call | solution.py:480

commit v8 on v7

--- a/solution.py
+++ b/solution.py
@@ -8,7 +8,7 @@
 MESH = pl.DeviceIdType.MESH
 SIDE = 4
 LAST = (320,)
-FIRST_WIDE, WIDE = 128, 176
+FIRST_WIDE, WIDE = 144, 144
 TILE_N = 768
 EXT_M = 160
 TOTAL_ROWS = 40960
@@ -18,7 +18,7 @@
 
 
 def gather_multiply(
-    coef, rot, c_buf, rms_out, scale, narrow, a_buf, r_buf, r2_buf, ext, sq_buf, sq_sum, sq_out, sq_in, scale_in,
+    coef, rot, result, rms_out, c_buf, scale, a_buf, r_buf, r2_buf, ext, sq_buf, sq_sum, sq_out, sq_in, scale_in,
     load_sem, a_sem, relay_sem, last_sem, r_sem, r2_sem, sems,
 ):
     rows, depth = coef.shape
@@ -48,7 +48,7 @@
         return pl.ds(pl.multiple_of(start, align), size)
 
     def a_part(block, by, start=0, size=None):
-        at = block * rows + shift(x, by) * quarter + start
+        at = (block * 3 + by + 1) * quarter + start
         return rows_at(at, quarter if size is None else size, 32)
 
     def piece_rows(at, cc, start=0, size=None):
@@ -58,8 +58,12 @@
 
     own_rot = pltpu.make_async_copy(rot, r_buf.at[piece_rows(own, core), :], load_sem.at[1])
     own_rot.start()
-    own_coef = pltpu.make_async_copy(coef, a_buf.at[rows_at(x * rows, rows), :], load_sem.at[0])
-    own_coef.start()
+
+    def own_part(by):
+        return coef.at[rows_at(shift(x, by) * quarter, quarter, 32), :]
+
+    for by in (-1, 0, 1):
+        pltpu.make_async_copy(own_part(by), a_buf.at[a_part(x, by), :], load_sem.at[0]).start()
 
     barrier = pltpu.get_barrier_semaphore()
     near = [(device_of(shift(z, by), y, core), x) for by in (1, -1)]
@@ -76,38 +80,42 @@
             device_id={"ga": ga, "ba": ba}, device_id_type=MESH,
         )
 
-    order = lambda by: (by, 2, 0)
-
-    def a_move(part, recv, to):
-        ref = a_buf.at[part, :]
-        return remote(ref, ref, sem["a_send"], recv, g, to)
+    def a_move(src, dst, recv, to):
+        src = src if isinstance(src, tuple) else (a_buf.at[src, :],)
+        return remote(src[0], a_buf.at[dst, :], sem["a_send"], recv, g, to)
 
     def a_start(direction, i):
         by = 1 - 2 * direction
-        a_move(a_part(x, order(by)[i]), a_sem.at[direction, i], shift(x, by)).start()
+        src = (a_part(x, by), (own_part(2),), a_part(x, 0))[i]
+        a_move(src, a_part(x, (0, by, -by)[i]), a_sem.at[direction, i], shift(x, by)).start()
 
     def a_wait(direction, i):
         by = 1 - 2 * direction
-        a_move(a_part(shift(x, -by), order(by)[i] - by), a_sem.at[direction, i], shift(x, by)).wait_recv()
+        part = a_part(shift(x, -by), (0, by, -by)[i])
+        a_move(part, part, a_sem.at[direction, i], shift(x, by)).wait_recv()
 
     def relay_start(direction):
         by = 1 - 2 * direction
-        a_move(a_part(shift(x, -by), 0), relay_sem.at[direction], shift(x, by)).start()
+        origin = shift(x, -by)
+        a_move(a_part(origin, 0), a_part(origin, -by), relay_sem.at[direction], shift(x, by)).start()
 
     def relay_wait(direction):
         by = 1 - 2 * direction
-        a_move(a_part(shift(x, 2), -by), relay_sem.at[direction], shift(x, by)).wait_recv()
+        part = a_part(shift(x, 2), -by)
+        a_move(part, part, relay_sem.at[direction], shift(x, by)).wait_recv()
 
     last_starts = [sum(LAST[:c]) for c in range(len(LAST))]
 
     def last_start(direction, c):
         by = 1 - 2 * direction
         size = LAST[c] // 2
-        part = a_part(shift(x, -by), by, last_starts[c] + direction * size, size)
-        a_move(part, last_sem.at[c], shift(x, by)).start()
+        start = last_starts[c] + direction * size
+        origin = shift(x, -by)
+        a_move(a_part(origin, by, start, size), a_part(origin, 0, start, size), last_sem.at[c], shift(x, by)).start()
 
     def last_wait(c):
-        a_move(a_part(shift(x, 2), 0, last_starts[c], LAST[c]), last_sem.at[c], shift(x, 1)).wait_recv()
+        part = a_part(shift(x, 2), 0, last_starts[c], LAST[c])
+        a_move(part, part, last_sem.at[c], shift(x, 1)).wait_recv()
 
     def place(h, first, second):
         return (shift(z, second), shift(y, first)) if h == 0 else (shift(z, first), shift(y, second))
@@ -284,7 +292,8 @@
         return r2_buf.at[pl.ds(h * (quarter - WIDE), count * (quarter - WIDE)), :]
 
     def rounded_copy(h):
-        dst = narrow.at[:, pl.ds(h * side_cols, side_cols)]
+        by = 1 - 2 * h
+        dst = result.at[rows_at(shift(x, -by) * quarter + WIDE, quarter - WIDE), pl.ds(h * side_cols, side_cols)]
         return remote(rounded(h), dst, sem["b_send"], sem["b_recv"], g, shift(x, 1 - 2 * h))
 
     def scale_copy(h):
@@ -306,7 +315,8 @@
             sem["x_send"], sem["x_recv"], g, shift(x, 2 * h - 1),
         ).start()
     r_own_first(0)
-    own_coef.wait()
+    loaded = a_buf.at[rows_at(x * 3 * quarter, 3 * quarter, 32), :]
+    pltpu.make_async_copy(loaded, loaded, load_sem.at[0]).wait()
     for i in range(3):
         for direction in (0, 1):
             a_start(direction, i)
@@ -401,39 +411,34 @@
     scale[...] = 1.0 / rms
     for h in (0, 1):
         scale_copy(h).start()
-        ext_copy(h, FIRST_WIDE, WIDE).start()
+        if FIRST_WIDE < WIDE:
+            ext_copy(h, FIRST_WIDE, WIDE).start()
     remote(scale, scale_in, sem["n_send"], sem["n_recv"], g, shift(x, 1)).wait()
     for h in (0, 1):
         rounded(h)[...] = (ext[h, WIDE:, :] * scale_in[:, h * side_cols:(h + 1) * side_cols]).astype(jnp.bfloat16)
         rounded_copy(h).start()
     ref = ext.at[:, pl.ds(0, WIDE), :]
     remote(ref, ref, sem["e_send"], sem["e_recv"], g, shift(x, 1)).wait()
+
+    def normalize(part):
+        result[part, :] = (c_buf[part, :] * scale[...]).astype(jnp.bfloat16)
+
+    normalize(rows_at(shift(x, 2) * quarter, WIDE))
+    for by in (-1, 0, 1):
+        normalize(rows_at(shift(x, by) * quarter, quarter))
     remote(rounded(0, 2), rounded(0, 2), sem["b_send"], sem["b_recv"], g, shift(x, 1)).wait()
 
 
-def normalize(c_buf, rms_in, scale, narrow, out, rms_out, staged, out_sem):
-    rows, cols = c_buf.shape
-    quarter = rows // SIDE
-    x = lax.axis_index("ba")
-    rms_out[...] = rms_in[...].reshape(cols)
+def put(result, rms_in, out, rms_out, rms, out_sem):
+    rows = result.shape[0]
     copies = []
-
-    def put(src, start, size):
-        part = pl.ds(pl.multiple_of(start, 16), size)
-        copy = pltpu.make_async_copy(src, out.at[part, :], out_sem.at[len(copies)])
-        copy.start()
-        copies.append(copy)
-
-    def opposite(by):
-        return (x + by) % SIDE * quarter
-
-    put(narrow, opposite(2) + WIDE, quarter - WIDE)
-    at = 0
-    for by, start, size in [(2, 0, WIDE)] + [(by, start, 64) for by in (0, 1, 3) for start in range(0, quarter, 64)]:
-        part = pl.ds(pl.multiple_of(opposite(by) + start, 64), size)
-        staged[pl.ds(at, size), :] = (c_buf[part, :] * scale[...]).astype(jnp.bfloat16)
-        put(staged.at[pl.ds(at, size), :], opposite(by) + start, size)
-        at += size
+    for i in range(4):
+        part = pl.ds(i * rows // 4, rows // 4)
+        copies.append(pltpu.make_async_copy(result.at[part, :], out.at[part, :], out_sem.at[i]))
+        copies[-1].start()
+    rms[...] = rms_in[...].reshape(rms.shape)
+    copies.append(pltpu.make_async_copy(rms, rms_out, out_sem.at[4]))
+    copies[-1].start()
     for copy in copies:
         copy.wait()
 
@@ -446,14 +451,13 @@
     row = pltpu.VMEM((1, cols), jnp.float32)
     parts = pl.pallas_call(
         gather_multiply,
-        out_shape=(
-            pltpu.VMEM((rows, cols), jnp.float32), row, row,
-            pltpu.VMEM((rows // SIDE - WIDE, cols), jnp.bfloat16),
-        ),
+        out_shape=(pltpu.VMEM((rows, cols), jnp.bfloat16), row),
         in_specs=[pl.BlockSpec(memory_space=pl.ANY)] * 2,
-        out_specs=(pl.BlockSpec(memory_space=pltpu.VMEM),) * 4,
+        out_specs=(pl.BlockSpec(memory_space=pltpu.VMEM),) * 2,
         scratch_shapes=[
-            pltpu.VMEM((SIDE * rows, depth), jnp.bfloat16),
+            pltpu.VMEM((rows, cols), jnp.float32),
+            row,
+            pltpu.VMEM((3 * rows, depth), jnp.bfloat16),
             pltpu.VMEM((SIDE * depth, cols), jnp.bfloat16),
             pltpu.VMEM((2 * SIDE * depth, cols // 2), jnp.bfloat16),
             pltpu.VMEM((2, rows // SIDE, cols // 2), jnp.float32),
@@ -471,25 +475,25 @@
             dma((len(SEMS),)),
         ],
         compiler_params=pltpu.CompilerParams(
-            collective_id=0, has_side_effects=True, vmem_limit_bytes=55 * 1024 * 1024
+            collective_id=0, has_side_effects=True, vmem_limit_bytes=60 * 1024 * 1024
         ),
         cost_estimate=pl.CostEstimate(
             flops=2 * rows * depth * SIDE * cols, bytes_accessed=4 * rows * depth, transcendentals=0
         ),
     )(coefficients, rotation)
     return pl.pallas_call(
-        normalize,
+        put,
         out_shape=(
             jax.ShapeDtypeStruct((rows, cols), jnp.bfloat16),
             jax.ShapeDtypeStruct((cols,), jnp.float32),
         ),
-        in_specs=[pl.BlockSpec(memory_space=pltpu.VMEM)] * 4,
-        out_specs=(pl.BlockSpec(memory_space=pl.ANY), pl.BlockSpec(memory_space=pltpu.VMEM)),
+        in_specs=[pl.BlockSpec(memory_space=pltpu.VMEM)] * 2,
+        out_specs=(pl.BlockSpec(memory_space=pl.ANY),) * 2,
         scratch_shapes=[
-            pltpu.VMEM((rows, cols), jnp.bfloat16),
-            dma((20,)),
+            pltpu.VMEM((cols,), jnp.float32),
+            dma((5,)),
         ],
-        compiler_params=pltpu.CompilerParams(vmem_limit_bytes=20 * 1024 * 1024),
+        compiler_params=pltpu.CompilerParams(vmem_limit_bytes=4 * 1024 * 1024),
         cost_estimate=pl.CostEstimate(flops=rows * cols, bytes_accessed=6 * rows * cols, transcendentals=0),
     )(*parts)
 

time: 133 us -> 132 us (level)
  no operation moved by 1% of the time
where the time goes in v8:
time: 132 us; the launch traced here: 131 us
  Pallas kernels  131 us (99%)
    pallas_call x1, Pallas kernels, body(): pl.pallas_call(gather_multiply, out_shape=(pltpu.VMEM((rows, cols), jnp.b...  129 us

profile of v8, /device:TPU:1, one launch (start us, length us, event | category | flops | bytes accessed | tf_op | source)
XLA Modules:
  0.0 131.5 jit_solution(14880774070857779229)
XLA Ops:
  0.6 128.9 %shard_map.41 = (bf16[1280,1536]{1,0:T(8,128)(2,1)S(1)}, f32[1,1536]{1,0:T(1,128)S(1)}) custom-call(bf16[1280,1536]{1,0:T(8,128)(2,1)} %coef.1, bf16[192,1536]{1,0:T(8,128)(2,1)} %rot.1), custom_call_target="tpu_custom_call" | custom-call | flops 24159191040 | bytes 7864320 | tf_op jit(solution)/shard_map/pallas_call | solution.py:452
  129.5 2.0 %shard_map.42 = (bf16[1280,1536]{1,0:T(8,128)(2,1)}, f32[1536]{0:T(1024)}) custom-call(bf16[1280,1536]{1,0:T(8,128)(2,1)S(1)} %get-tuple-element.4.result, f32[1,1536]{1,0:T(1,128)S(1)} %get-tuple-element.5.rms_in), custom_call_target="tpu_custom_call" | custom-call | flops 1966080 | bytes 11796480 | tf_op jit(solution)/shard_map/pallas_call | solution.py:484

commit v9 on v8

--- a/solution.py
+++ b/solution.py
@@ -8,7 +8,7 @@
 MESH = pl.DeviceIdType.MESH
 SIDE = 4
 LAST = (320,)
-FIRST_WIDE, WIDE = 144, 144
+FIRST_WIDE, WIDE = 144, 176
 TILE_N = 768
 EXT_M = 160
 TOTAL_ROWS = 40960
@@ -284,7 +284,7 @@
 
     def ext_copy(h, start, stop):
         by = 1 - 2 * h
-        dst = c_buf.at[rows_at(shift(x, -by) * quarter + start, stop - start, 64), pl.ds(h * side_cols, side_cols)]
+        dst = c_buf.at[rows_at(shift(x, -by) * quarter + start, stop - start), pl.ds(h * side_cols, side_cols)]
         src = ext.at[h, pl.ds(start, stop - start), :]
         return remote(src, dst, sem["e_send"], sem["e_recv"], g, shift(x, by))
 
@@ -411,8 +411,8 @@
     scale[...] = 1.0 / rms
     for h in (0, 1):
         scale_copy(h).start()
-        if FIRST_WIDE < WIDE:
-            ext_copy(h, FIRST_WIDE, WIDE).start()
+    for h in (0, 1):
+        ext_copy(h, FIRST_WIDE, WIDE).start()
     remote(scale, scale_in, sem["n_send"], sem["n_recv"], g, shift(x, 1)).wait()
     for h in (0, 1):
         rounded(h)[...] = (ext[h, WIDE:, :] * scale_in[:, h * side_cols:(h + 1) * side_cols]).astype(jnp.bfloat16)

time: 132 us -> 131 us (level)
  no operation moved by 1% of the time
where the time goes in v9:
time: 131 us; the launch traced here: 130 us
  Pallas kernels  130 us (99%)
    pallas_call x1, Pallas kernels, body(): pl.pallas_call(gather_multiply, out_shape=(pltpu.VMEM((rows, cols), jnp.b...  128 us

profile of v9, /device:TPU:1, one launch (start us, length us, event | category | flops | bytes accessed | tf_op | source)
XLA Modules:
  0.0 130.3 jit_solution(17448354077464016263)
XLA Ops:
  0.6 127.7 %shard_map.41 = (bf16[1280,1536]{1,0:T(8,128)(2,1)S(1)}, f32[1,1536]{1,0:T(1,128)S(1)}) custom-call(bf16[1280,1536]{1,0:T(8,128)(2,1)} %coef.1, bf16[192,1536]{1,0:T(8,128)(2,1)} %rot.1), custom_call_target="tpu_custom_call" | custom-call | flops 24159191040 | bytes 7864320 | tf_op jit(solution)/shard_map/pallas_call | solution.py:452
  128.4 2.0 %shard_map.42 = (bf16[1280,1536]{1,0:T(8,128)(2,1)}, f32[1536]{0:T(1024)}) custom-call(bf16[1280,1536]{1,0:T(8,128)(2,1)S(1)} %get-tuple-element.4.result, f32[1,1536]{1,0:T(1,128)S(1)} %get-tuple-element.5.rms_in), custom_call_target="tpu_custom_call" | custom-call | flops 1966080 | bytes 11796480 | tf_op jit(solution)/shard_map/pallas_call | solution.py:484

commit v10 on v9

--- a/solution.py
+++ b/solution.py
@@ -7,7 +7,7 @@
 
 MESH = pl.DeviceIdType.MESH
 SIDE = 4
-LAST = (320,)
+LAST = (192, 128)
 FIRST_WIDE, WIDE = 144, 176
 TILE_N = 768
 EXT_M = 160
@@ -213,8 +213,10 @@
         size = quarter if size is None else size
         out_rows = rows_at(shift(x, by) * quarter + start, size, 32)
 
+        tile = cols if mode == "last" else TILE_N
+
         def step(j, carry):
-            columns = pl.ds(pl.multiple_of(j * TILE_N, TILE_N), TILE_N)
+            columns = pl.ds(pl.multiple_of(j * tile, tile), tile)
             value = product(k, by, start, size, columns)
             if mode != "set":
                 value = value + c_buf[out_rows, columns]
@@ -223,7 +225,7 @@
                 sq_sum[:, columns] += jnp.sum(value * value, axis=0, keepdims=True)
             return carry
 
-        lax.fori_loop(0, cols // TILE_N, step, 0)
+        lax.fori_loop(0, cols // tile, step, 0)
 
     delta = (x + 2 - z + SIDE) % SIDE
     low = 1 - delta // 2

time: 131 us -> 130 us (level)
  no operation moved by 1% of the time
where the time goes in v10:
time: 130 us; the launch traced here: 129 us
  Pallas kernels  129 us (99%)
    pallas_call x1, Pallas kernels, body(): pl.pallas_call(gather_multiply, out_shape=(pltpu.VMEM((rows, cols), jnp.b...  127 us

profile of v10, /device:TPU:1, one launch (start us, length us, event | category | flops | bytes accessed | tf_op | source)
XLA Modules:
  0.0 129.3 jit_solution(14144194228936402453)
XLA Ops:
  0.6 126.7 %shard_map.41 = (bf16[1280,1536]{1,0:T(8,128)(2,1)S(1)}, f32[1,1536]{1,0:T(1,128)S(1)}) custom-call(bf16[1280,1536]{1,0:T(8,128)(2,1)} %coef.1, bf16[192,1536]{1,0:T(8,128)(2,1)} %rot.1), custom_call_target="tpu_custom_call" | custom-call | flops 24159191040 | bytes 7864320 | tf_op jit(solution)/shard_map/pallas_call | solution.py:454
  127.4 2.0 %shard_map.42 = (bf16[1280,1536]{1,0:T(8,128)(2,1)}, f32[1536]{0:T(1024)}) custom-call(bf16[1280,1536]{1,0:T(8,128)(2,1)S(1)} %get-tuple-element.4.result, f32[1,1536]{1,0:T(1,128)S(1)} %get-tuple-element.5.rms_in), custom_call_target="tpu_custom_call" | custom-call | flops 1966080 | bytes 11796480 | tf_op jit(solution)/shard_map/pallas_call | solution.py:486

commit v11 on v10

--- a/solution.py
+++ b/solution.py
@@ -140,9 +140,11 @@
         recv = (r_sem if q == 0 else r2_sem).at[h, slot]
         remote(ref, ref, sem["r_send"] if q == 0 else sem["r2_send"], recv, device_of(to[0], to[1], core), x).start()
 
-    def r_wait(q, h, at, slot):
-        ref = r_ref(q, h, at, None, core)
-        recv = (r_sem if q == 0 else r2_sem).at[h, slot]
+    def r_wait(q, h, slot, count):
+        if q == 0:
+            ref, recv = r_buf.at[pl.ds(0, count * (piece // 2)), :], r_sem.at[h, slot]
+        else:
+            ref, recv = r2_buf.at[pl.ds(0, count * piece), :], r2_sem.at[h, slot]
         remote(ref, ref, sem["r_send"], recv, partner, x).wait_recv()
 
     def to_partner(q, h, at, late):
@@ -152,17 +154,17 @@
 
     places = {0: 0, -1: 1, 1: 2, 2: 3}
 
-    def slot_of(first, kind):
-        return 3 + 3 * places[first] + kind
+    def slot_of(first, opposite):
+        return 2 + 4 * opposite + places[first]
 
     def along_second(q, h, at, first):
         for direction in (0, 1):
-            r_start(q, h, at, None, slot_of(first, direction), place(h, 0, 1 - 2 * direction))
+            r_start(q, h, at, None, slot_of(first, 0), place(h, 0, 1 - 2 * direction))
 
     def r_own_first(q):
         for h in (0, 1):
             for direction in (0, 1):
-                r_start(q, h, own, None, direction, place(h, 1 - 2 * direction, 0))
+                r_start(q, h, own, None, 0, place(h, 1 - 2 * direction, 0))
 
     def r_own_second(q):
         for h in (0, 1):
@@ -170,12 +172,10 @@
             to_partner(q, h, own, 0)
 
     def r_first(q):
-        for direction in (0, 1):
-            by = 1 - 2 * direction
-            for h in (0, 1):
-                at = place(h, -by, 0)
-                r_wait(q, h, at, direction)
-                r_start(q, h, at, direction, 2, place(h, by, 0))
+        for h in (0, 1):
+            r_wait(q, h, 0, 2)
+            for direction, by in ((0, 1), (1, -1)):
+                r_start(q, h, place(h, -by, 0), direction, 1, place(h, by, 0))
         for by in (1, -1):
             for h in (0, 1):
                 at = place(h, -by, 0)
@@ -184,20 +184,20 @@
 
     def r_opposite(q, h):
         at = place(h, 2, 0)
-        r_wait(q, h, at, 2)
+        r_wait(q, h, 1, 1)
         along_second(q, h, at, 2)
         to_partner(q, h, at, 0)
 
-    def r_second(q, first, direction, h):
-        by = 1 - 2 * direction
-        at = place(h, first, -by)
-        r_wait(q, h, at, slot_of(first, direction))
-        r_start(q, h, at, direction, slot_of(first, 2), place(h, 0, by))
-        to_partner(q, h, at, 0)
+    def r_second(q, first, h):
+        r_wait(q, h, slot_of(first, 0), 2)
+        for direction, by in ((0, 1), (1, -1)):
+            at = place(h, first, -by)
+            r_start(q, h, at, direction, slot_of(first, 1), place(h, 0, by))
+            to_partner(q, h, at, 0)
 
     def r_second_opposite(q, first, h):
         at = place(h, first, 2)
-        r_wait(q, h, at, slot_of(first, 2))
+        r_wait(q, h, slot_of(first, 1), 1)
         to_partner(q, h, at, 1)
 
     FIRSTS = (0, -1, 1, 2)
@@ -329,9 +329,8 @@
     for h in (0, 1):
         r_opposite(0, h)
     for first in FIRSTS:
-        for direction in (0, 1):
-            for h in (0, 1):
-                r_second(0, first, direction, h)
+        for h in (0, 1):
+            r_second(0, first, h)
     two = r2_buf.at[pl.ds(0, 2 * piece), :]
     remote(two, two, sem["x_send"], sem["x_recv"], g, shift(x, 1)).wait()
     r_own_first(1)
@@ -361,9 +360,8 @@
         unit(k, -k, "add")
     r_opposite(1, 1)
     for first in FIRSTS:
-        for direction in (0, 1):
-            for h in (0, 1):
-                r_second(1, first, direction, h)
+        for h in (0, 1):
+            r_second(1, first, h)
         if first == 0:
             for direction, k in enumerate((-1, 1)):
                 a_wait(direction, 2)
@@ -472,8 +470,8 @@
             dma((2, 3)),
             dma((2,)),
             dma((len(LAST),)),
-            dma((2, 15)),
-            dma((2, 15)),
+            dma((2, 10)),
+            dma((2, 10)),
             dma((len(SEMS),)),
         ],
         compiler_params=pltpu.CompilerParams(

time: 130 us -> 130 us (level)
  no operation moved by 1% of the time
where the time goes in v11:
time: 130 us; the launch traced here: 129 us
  Pallas kernels  128 us (98%)
    pallas_call x1, Pallas kernels, body(): pl.pallas_call(gather_multiply, out_shape=(pltpu.VMEM((rows, cols), jnp.b...  127 us

profile of v11, /device:TPU:1, one launch (start us, length us, event | category | flops | bytes accessed | tf_op | source)
XLA Modules:
  0.0 129.1 jit_solution(13219998056810020740)
XLA Ops:
  0.6 126.5 %shard_map.41 = (bf16[1280,1536]{1,0:T(8,128)(2,1)S(1)}, f32[1,1536]{1,0:T(1,128)S(1)}) custom-call(bf16[1280,1536]{1,0:T(8,128)(2,1)} %coef.1, bf16[192,1536]{1,0:T(8,128)(2,1)} %rot.1), custom_call_target="tpu_custom_call" | custom-call | flops 24159191040 | bytes 7864320 | tf_op jit(solution)/shard_map/pallas_call | solution.py:452
  127.2 2.0 %shard_map.42 = (bf16[1280,1536]{1,0:T(8,128)(2,1)}, f32[1536]{0:T(1024)}) custom-call(bf16[1280,1536]{1,0:T(8,128)(2,1)S(1)} %get-tuple-element.4.result, f32[1,1536]{1,0:T(1,128)S(1)} %get-tuple-element.5.rms_in), custom_call_target="tpu_custom_call" | custom-call | flops 1966080 | bytes 11796480 | tf_op jit(solution)/shard_map/pallas_call | solution.py:484

commit v12 on v11

--- a/solution.py
+++ b/solution.py
@@ -9,7 +9,6 @@
 SIDE = 4
 LAST = (192, 128)
 FIRST_WIDE, WIDE = 144, 176
-TILE_N = 768
 EXT_M = 160
 TOTAL_ROWS = 40960
 SENDS = ("a_send", "r_send", "r2_send", "p_send", "p2_send", "x_send", "e_send", "q_send", "s_send", "n_send", "b_send")
@@ -213,7 +212,7 @@
         size = quarter if size is None else size
         out_rows = rows_at(shift(x, by) * quarter + start, size, 32)
 
-        tile = cols if mode == "last" else TILE_N
+        tile = cols
 
         def step(j, carry):
             columns = pl.ds(pl.multiple_of(j * tile, tile), tile)

time: 130 us -> 130 us (level)
  no operation moved by 1% of the time
where the time goes in v12:
time: 130 us; the launch traced here: 129 us
  Pallas kernels  128 us (98%)
    pallas_call x1, Pallas kernels, body(): pl.pallas_call(gather_multiply, out_shape=(pltpu.VMEM((rows, cols), jnp.b...  127 us

profile of v12, /device:TPU:1, one launch (start us, length us, event | category | flops | bytes accessed | tf_op | source)
XLA Modules:
  0.0 129.3 jit_solution(4802908686059444929)
XLA Ops:
  0.6 126.5 %shard_map.41 = (bf16[1280,1536]{1,0:T(8,128)(2,1)S(1)}, f32[1,1536]{1,0:T(1,128)S(1)}) custom-call(bf16[1280,1536]{1,0:T(8,128)(2,1)} %coef.1, bf16[192,1536]{1,0:T(8,128)(2,1)} %rot.1), custom_call_target="tpu_custom_call" | custom-call | flops 24159191040 | bytes 7864320 | tf_op jit(solution)/shard_map/pallas_call | solution.py:451
  127.2 2.0 %shard_map.42 = (bf16[1280,1536]{1,0:T(8,128)(2,1)}, f32[1536]{0:T(1024)}) custom-call(bf16[1280,1536]{1,0:T(8,128)(2,1)S(1)} %get-tuple-element.4.result, f32[1,1536]{1,0:T(1,128)S(1)} %get-tuple-element.5.rms_in), custom_call_target="tpu_custom_call" | custom-call | flops 1966080 | bytes 11796480 | tf_op jit(solution)/shard_map/pallas_call | solution.py:483
